TPU v7x, 512 devices: a whole 4x8x8 slice. The times are simulated.
512 devices in a mesh: dp: 16 (over y_lo, x), space: 32 (over z, y_hi, core).
Axes of the slice: x: 4, y: 8 (y_hi: 2, y_lo: 4; y = y_hi * 4 + y_lo), z: 8, core: 2. Of those that a mesh axis runs over, the one named last changes fastest.
Arguments:
- fields: bfloat16 [16, 100, 131072], P('dp', None, 'space'), may hold values from -6 to 6
- cell_index: int32 [1024, 128], P('space'), may hold values from 0 to 6143
- interp_weight: bfloat16 [1024, 16, 128], P('space'), may hold values from 0 to 2, as said below
- w_in: bfloat16 [100, 1024], replicated, may hold values from -0.625 to 0.625
- ln_gain: float32 [1024], replicated, may hold values from 0.5 to 1.5
- w_qkv: bfloat16 [1024, 3072], P('dp'), may hold values from -0.1875 to 0.1875
- w_out: bfloat16 [1024, 1024], P('dp'), may hold values from -3 to 3
Outputs:
- latent: bfloat16 [16, 16384, 1024], P('dp', 'space')
- update: bfloat16 [16, 16384, 1024], P('dp', 'space')
Inputs may be any that keep to these rules, and one draw needn't show every extreme that they name: `interp_weight`: in each block the slots from some count on carry zero weight for all its 16 nodes; that count lies between 48 and 128. `cell_index`: indexes a shard's 4096 cells extended by 1024 cells of each neighbouring shard, lower neighbour first.
All inputs are finite; a program needn't handle non-finite values.
Results may differ from a plain program's by a relative error of at most 0.0068.
Values may be sent and summed in bfloat16 or wider, within the bound.
No kernel may reach another device: no remote copies, remote signals or barrier semaphores. Data moves between devices by JAX's collectives and lax.ppermute only.
A program may use at most 128 MiB of HBM per device.

v0:
```python
import math

import jax
import jax.numpy as jnp
from jax import lax
from jax.experimental import pallas as pl
from jax.experimental.layout import Layout, with_layout_constraint
from jax.experimental.pallas import tpu as pltpu
from jax.sharding import PartitionSpec as P


BF, F32 = jnp.bfloat16, jnp.float32
AXES = ("dp", "space")


def coords(dp, s):
    return dp % 4, (s // 2 % 2) * 4 + dp // 4, s // 4, s % 2


def index(x, y, z, c):
    x, y, z = x % 4, y % 8, z % 8
    return ((y % 4) * 4 + x) * 32 + z * 4 + (y // 4) * 2 + c


def send(array, move):
    pairs = [
        (dp * 32 + s, index(*move(*coords(dp, s)))) for dp in range(16) for s in range(32)
    ]
    return lax.ppermute(array, AXES, pairs)


def along(first, shift):
    def move(x, y, z, c):
        return (shift(x), y, z, c) if (c == 0) == first else (x, shift(y), z, c)

    return move


def two(place):
    return place - 2 if place % 2 else place + 2


STEPS = (lambda i: i + 1, lambda i: i - 1, two)
SOURCES = (0, 3, 1, 2)


def swap(array):
    return send(array, lambda x, y, z, c: (x, y, z, 1 - c))


def ring(array, move):
    return lax.ppermute(array, "space", [(s, move(s) % 32) for s in range(32)])


def neighbour(array):
    return ring(array, lambda s: s + 1 if s % 2 else s - 1)


def row_major(array):
    return with_layout_constraint(array, Layout(major_to_minor=(0, 1)))


def call(kernel, outs, scratch, flops, limit, n_in, aliases={}, n_smem=1):
    return pl.pallas_call(
        kernel,
        out_shape=[jax.ShapeDtypeStruct(s, d) for s, d in outs],
        in_specs=[pl.BlockSpec(memory_space=pltpu.SMEM)] * n_smem
        + [pl.BlockSpec(memory_space=pltpu.VMEM)] * n_in,
        out_specs=[pl.BlockSpec(memory_space=pltpu.VMEM)] * len(outs),
        scratch_shapes=[pltpu.VMEM(s, d) for s, d in scratch],
        compiler_params=pltpu.CompilerParams(vmem_limit_bytes=limit << 20),
        cost_estimate=pl.CostEstimate(flops=flops, bytes_accessed=1 << 20, transcendentals=0),
        input_output_aliases=aliases,
    )


def rows_at(start, count=256):
    return pl.ds(pl.multiple_of(start, 256), count)


def dot(a, b):
    return jnp.dot(a, b, preferred_element_type=F32)


def turn(cells, start, table, tall):
    count = cells.shape[1]
    tall[:100, :count] = cells[...].astype(F32)
    for j in range(0, count, 128):
        table[pl.ds(pl.multiple_of(start + j, 128), 128), :] = tall[:, j : j + 128].T


def table_kernel(where, cells, table, tall):
    tall[96:, :] = jnp.zeros((32, 1024), F32)

    def part(i, carry):
        at = pl.multiple_of(i * 1024, 1024)
        turn(cells.at[:, pl.ds(at, 1024)], at + 1024, table, tall)
        return carry

    lax.fori_loop(0, 4, part, 0)


def encode_blocks(start, index, weight, table, out, picked):
    live = lax.broadcasted_iota(jnp.int32, (16, 128), 1) < 100

    def pair(i, carry):
        for half in range(2):
            local = i * 2 + half
            b = start + local
            for j in range(128):
                picked[half, j : j + 1, :] = table[pl.ds(index[b, j], 1), :]
            summed = dot(weight[b], picked[half].astype(BF))
            rows = pl.ds(pl.multiple_of(local * 16, 16), 16)
            out[rows, :] = jnp.where(live, summed, 0.0).astype(BF)
        return carry

    lax.fori_loop(0, 8, pair, 0)


def encode_edge_kernel(where, index, weight, near, mate, filled, out, table, tall, picked):
    core = where[0]
    tall[96:, :] = jnp.zeros((32, 1024), F32)
    turn(near, core * 5120, table, tall)
    turn(mate, 5120 - core * 5120, table, tall)
    encode_blocks(core * 16, index, weight, table, out, picked)


def encode_inner_kernel(where, index, weight, table, out, picked):
    encode_blocks(16 - where[0] * 16, index, weight, table, out, picked)


def normalised(encoded, w_in, gain):
    embedded = dot(encoded, w_in)
    average = jnp.mean(embedded, axis=1, keepdims=True)
    centered = embedded - average
    spread = jnp.mean(centered * centered, axis=1, keepdims=True)
    return embedded, (centered * lax.rsqrt(spread + 1e-05) * gain).astype(BF)


def widen(w_in, wide):
    wide[96:, :] = jnp.zeros((32, 1024), BF)
    wide[:100, :] = w_in[...]


def embed_own_kernel(where, edge, inner, w_in, gain, normed, latent, wide):
    widen(w_in, wide)
    at = where[0] * 256
    for piece, start in ((edge, at), (inner, 256 - at)):
        embedded, unit = normalised(piece[...], wide[...], gain[...])
        normed[rows_at(start), :] = unit
        latent[rows_at(start), :] = embedded.astype(BF)


def embed_rest_kernel(where, near, mate, w_in, gain, normed, wide):
    widen(w_in, wide)
    at = where[0] * 256
    for piece, start in ((mate[:256], 256 - at), (mate[256:512], at), (mate[512:], 512), (near[...], 768)):
        _, unit = normalised(piece, wide[...], gain[...])
        normed[rows_at(start), :] = unit


def head_ones():
    same = lax.broadcasted_iota(jnp.int32, (256, 256), 0) // 64 == (
        lax.broadcasted_iota(jnp.int32, (256, 256), 1) // 64
    )
    return jnp.where(same, 1.0, 0.0).astype(BF)


def unit_heads(rows, ones, ref, at):
    for h in range(2):
        part = rows[:, h * 256 : (h + 1) * 256]
        squares = dot((part * part).astype(BF), ones)
        unit = (part * lax.rsqrt(squares * (1.0 / 64) + 1e-06)).astype(BF)
        ref[2 * h, at, :] = unit[:, :128]
        ref[2 * h + 1, at, :] = unit[:, 128:]


def project_tile(rows, weights, ones, q, k, v, q_at, k_at):
    unit_heads(dot(rows, weights[:, 512:1024]), ones, k, k_at)
    values = dot(rows, weights[:, 1024:1536]).astype(BF)
    for p in range(4):
        v[p, k_at, :] = values[:, p * 128 : (p + 1) * 128]
    if q_at is not None:
        unit_heads(dot(rows, weights[:, :512]), ones, q, q_at)


def project_own_kernel(where, normed, own, before, after, across, q, k, v, out_rows, weights):
    core, x, y = where[0], where[1], where[2]
    first, second = jnp.where(core == 0, x, y), jnp.where(core == 0, y, x)
    for step, piece in zip(SOURCES, (own, before, after, across)):
        other = lax.rem(second + step, 4)
        for m in range(4):
            mine = lax.rem(first + SOURCES[m], 4)
            block = jnp.where(core == 0, other * 4 + mine, mine * 4 + other)
            rows = pl.ds(pl.multiple_of(block * 64, 64), 64)
            weights[rows, :] = piece[m * 64 : (m + 1) * 64, :1536]
            out_rows[rows, :] = piece[m * 64 : (m + 1) * 64, 1536:]
    ones = head_ones()
    start = core * 512
    for i in range(0, 512, 256):
        rows = normed[i : i + 256, :]
        project_tile(rows, weights, ones, q, k, v, rows_at(start + i), rows_at(start + i + 256))


def project_rest_kernel(where, normed, weights, q_in, k_in, v_in, q, k, v):
    core = where[0]
    ones = head_ones()
    start = 512 - core * 512
    for i in range(0, 512, 256):
        rows = normed[i : i + 256, :]
        project_tile(rows, weights, ones, q, k, v, rows_at(start + i), rows_at(start + i + 256))
    for i, at in ((512, 1280 - core * 1280), (768, core * 1280)):
        project_tile(normed[i : i + 256, :], weights, ones, q, k, v, None, rows_at(at))


def attend_kernel(shard, q, k, v, out):
    scale = math.log2(math.e) / 8.0
    low = lax.broadcasted_iota(jnp.int32, (512, 128), 1) < 64
    start = pl.multiple_of(shard[0] * 512, 512)

    def tile(p, carry):
        query = q[p, pl.ds(start, 512), :]
        zero = jnp.zeros_like(query)
        heads = (jnp.where(low, query, zero), jnp.where(low, zero, query))
        both = [None, None]
        for at in range(0, 1024, 256):
            keys = k[p, pl.ds(start + at, 256), :]
            wide = jnp.concatenate(
                [v[p, pl.ds(start + at, 256), :], jnp.ones((256, 128), BF)], axis=1
            )
            for h, head in enumerate(heads):
                scores = lax.dot_general(
                    head, keys, (((1,), (1,)), ((), ())), preferred_element_type=F32
                )
                part = dot(jnp.exp2(scores * scale).astype(BF), wide)
                both[h] = part if at == 0 else both[h] + part
        mixed = [b[:, :128] / b[:, 128:] for b in both]
        out[p, :, :] = jnp.where(low, mixed[0], mixed[1]).astype(BF)
        return carry

    lax.fori_loop(0, 4, tile, 0)


def out_kernel(where, mine, theirs, rows, update):
    core = where[0]
    join = lambda ref: jnp.concatenate([ref[p] for p in range(4)], axis=1)
    near = rows[pl.ds(pl.multiple_of(core * 512, 512), 512), :]
    far = rows[pl.ds(pl.multiple_of(512 - core * 512, 512), 512), :]
    update[...] = (dot(join(mine), near) + dot(join(theirs), far)).astype(BF)


def shards(fields, cell_index, interp_weight, w_in, ln_gain, w_qkv, w_out):
    dp, space = lax.axis_index("dp"), lax.axis_index("space")
    core = lax.rem(space, 2)
    slot = lax.iota(jnp.int32, 4)
    where = jnp.where(slot == 0, core, jnp.where(slot == 1, lax.rem(dp, 4), lax.div(dp, 4)))

    even = core == 0
    grid_field = fields[0]
    first, last = grid_field[:, :1024], grid_field[:, 3072:]
    near_cells = row_major(neighbour(row_major(jnp.where(even, first, last))))
    mate_cells = row_major(swap(row_major(jnp.where(even, last, first))))

    halves = [
        jnp.where(even, w[:, i : i + 512], w[:, i + 512 : i + 1024])
        for w, i in ((w_qkv, 0), (w_qkv, 1024), (w_qkv, 2048))
    ]
    block = jnp.concatenate(halves + [w_out], axis=1)
    line = [block]
    for shift in STEPS:
        line.append(send(block, along(True, shift)))
    group = jnp.concatenate(line, axis=0)
    gathered = [group]
    for shift in STEPS:
        gathered.append(send(group, along(False, shift)))

    grown = ((6144, 128), F32)
    tall = ((128, 1024), F32)
    (table,) = call(table_kernel, [grown], [tall], 2_000_000_000, 8, 1)(
        where, grid_field
    )
    picked = ((2, 128, 128), F32)
    part = ((256, 128), BF)
    edge, table = call(
        encode_edge_kernel, [part, grown], [tall, picked], 3_000_000_000, 8, 4, {5: 1}, 2
    )(where, cell_index, interp_weight, near_cells, mate_cells, table)
    near = neighbour(edge)
    (inner,) = call(encode_inner_kernel, [part], [picked], 3_000_000_000, 8, 2, {}, 2)(
        where, cell_index, interp_weight, table
    )
    mate = swap(jnp.concatenate([edge, inner, near], axis=0))

    gain = ln_gain[None]
    wide = [((128, 1024), BF)]
    own_normed, latent = call(
        embed_own_kernel, [((512, 1024), BF), ((512, 1024), BF)], wide, 1_500_000_000, 12, 4
    )(where, edge, inner, w_in, gain)
    (rest_normed,) = call(
        embed_rest_kernel, [((1024, 1024), BF)], wide, 3_000_000_000, 12, 4
    )(where, near, mate, w_in, gain)
    shapes = [((4, 1024, 128), BF), ((4, 1536, 128), BF), ((4, 1536, 128), BF)]
    q, k, v, out_rows, weights = call(
        project_own_kernel,
        shapes + [((1024, 1024), BF), ((1024, 1536), BF)],
        [],
        3_000_000_000,
        12,
        5,
    )(where, own_normed, *gathered)
    q, k, v = call(
        project_rest_kernel, shapes, [], 5_000_000_000, 12, 5, {3: 0, 4: 1, 5: 2}
    )(where, rest_normed, weights, q, k, v)
    attend = call(attend_kernel, [((4, 512, 128), BF)], [], 8_000_000_000, 16, 3)
    (other,) = attend((1 - core)[None], q, k, v)
    theirs = swap(other)
    (mine,) = attend(core[None], q, k, v)
    (update,) = call(out_kernel, [((512, 1024), BF)], [], 1_000_000_000, 8, 3)(
        where, mine, theirs, out_rows
    )
    return latent[None], update[None]


def solution(mesh):
    placed = (
        P("dp", None, "space"),
        P("space", None),
        P("space", None, None),
        P(),
        P(),
        P("dp", None),
        P("dp", None),
    )
    return jax.shard_map(
        shards,
        mesh=mesh,
        in_specs=placed,
        out_specs=(P("dp", "space", None), P("dp", "space", None)),
        check_vma=False,
    )
```

profile of v0, /device:TPU:27, one launch (start us, length us, event | category | flops | bytes accessed | tf_op | source)
XLA Modules:
  0.0 100.1 jit_solution(12199333738141743804)
XLA Ops:
  0.6 0.0 copy-start.5
  0.6 1.1 %slice_select_fusion.2 = (bf16[64,512]{1,0:T(8,128)(2,1)S(1)}, bf16[64,512]{1,0:T(8,128)(2,1)S(1)}, bf16[64,512]{1,0:T(8,128)(2,1)S(1)}) fusion(bf16[64,3072]{1,0:T(8,128)(2,1)} %param.12, pred[]{:T(512)S(6)} %eq.11), kind=kLoop, calls=%fused_computation.7 | loop fusion | flops 98304 | bytes 589825 | tf_op jit(solution)/shard_map/jit(_where)/select_n | solution.py:265
  1.7 0.0 copy-start
  1.7 1.0 %pad_maximum_fusion.1 = bf16[64,2560]{1,0:T(8,128)(2,1)S(1)} fusion(bf16[64,1024]{1,0:T(8,128)(2,1)} %param.13, bf16[64,512]{1,0:T(8,128)(2,1)S(1)} %get-tuple-element.29, bf16[64,512]{1,0:T(8,128)(2,1)S(1)} %get-tuple-element.30, bf16[64,512]{1,0:T(8,128)(2,1)S(1)} %get-tuple-element.28), kind=kLoop, calls=%fused_computation.1 | loop fusion | flops 1310720 | bytes 655360 | tf_op jit(solution)/shard_map/concatenate | solution.py:268
  2.7 4.4 %collective-permute-start.4 = (bf16[64,2560]{1,0:T(8,128)(2,1)S(1)}, bf16[64,2560]{1,0:T(8,128)(2,1)S(1)}, u32[]{:S(2)}, u32[]{:S(2)}) collective-permute-start(bf16[64,2560]{1,0:T(8,128)(2,1)S(1)} %pad_maximum_fusion.1), channel_id=1, source_target_pairs={{0,32},{1,129},{2,34},{3,131},{4,36},{5,133},{6,38},{7,135},{8,40}... | collective-permute-start | bytes 983048 | tf_op jit(solution)/shard_map/ppermute | solution.py:29
  7.2 1.9 %collective-permute-start.5 = (bf16[64,2560]{1,0:T(8,128)(2,1)S(1)}, bf16[64,2560]{1,0:T(8,128)(2,1)S(1)}, u32[]{:S(2)}, u32[]{:S(2)}) collective-permute-start(bf16[64,2560]{1,0:T(8,128)(2,1)S(1)} %pad_maximum_fusion.1), channel_id=1, source_target_pairs={{0,96},{1,387},{2,98},{3,385},{4,100},{5,391},{6,102},{7,389},{8,1... | collective-permute-start | bytes 983048 | tf_op jit(solution)/shard_map/ppermute | solution.py:29
  9.1 1.9 %collective-permute-start.6 = (bf16[64,2560]{1,0:T(8,128)(2,1)S(1)}, bf16[64,2560]{1,0:T(8,128)(2,1)S(1)}, u32[]{:S(2)}, u32[]{:S(2)}) collective-permute-start(bf16[64,2560]{1,0:T(8,128)(2,1)S(1)} %pad_maximum_fusion.1), channel_id=1, source_target_pairs={{0,64},{1,257},{2,66},{3,259},{4,68},{5,261},{6,70},{7,263},{8,72}... | collective-permute-start | bytes 983048 | tf_op jit(solution)/shard_map/ppermute | solution.py:29
  11.0 1.8 %broadcast_select_fusion = (bf16[100,1024]{1,0:T(8,128)(2,1)}, bf16[100,1024]{1,0:T(8,128)(2,1)}) fusion(pred[]{:T(512)S(6)} %eq.11, bf16[100,4096]{1,0:T(8,128)(2,1)} %bitcast.6), kind=kLoop, calls=%fused_computation.2 | loop fusion | flops 204800 | bytes 819201 | tf_op jit(solution)/shard_map/jit(_where)/select_n | solution.py:262
  12.8 6.9 %collective-permute-start = (bf16[100,1024]{1,0:T(8,128)(2,1)}, bf16[100,1024]{1,0:T(8,128)(2,1)}, u32[]{:S(2)}, u32[]{:S(2)}) collective-permute-start(bf16[100,1024]{1,0:T(8,128)(2,1)} %get-tuple-element.27), channel_id=1, source_target_pairs={{0,31},{1,2},{2,1},{3,4},{4,3},{5,6},{6,5},{7,8},{8,7},{9,10},{10,... | collective-permute-start | bytes 614408 | tf_op jit(solution)/shard_map/ppermute | solution.py:52
  19.8 9.4 %collective-permute-start.1 = (bf16[100,1024]{1,0:T(8,128)(2,1)}, bf16[100,1024]{1,0:T(8,128)(2,1)}, u32[]{:S(2)}, u32[]{:S(2)}) collective-permute-start(bf16[100,1024]{1,0:T(8,128)(2,1)} %get-tuple-element.26), channel_id=1, source_target_pairs={{0,1},{1,0},{2,3},{3,2},{4,5},{5,4},{6,7},{7,6},{8,9},{9,8},{10,11... | collective-permute-start | bytes 614408 | tf_op jit(solution)/shard_map/ppermute | solution.py:29
  29.2 0.0 collective-permute-done.4
  29.2 0.0 collective-permute-done.5
  29.2 0.0 collective-permute-done.6
  29.2 0.0 copy-done.5
  29.2 0.1 pad_maximum_fusion.own
  29.3 0.0 copy-start.2
  29.3 0.0 copy-start.3
  29.3 3.3 %collective-permute-start.7 = (bf16[256,2560]{1,0:T(8,128)(2,1)S(1)}, bf16[256,2560]{1,0:T(8,128)(2,1)S(1)}, u32[]{:S(2)}, u32[]{:S(2)}) collective-permute-start(bf16[256,2560]{1,0:T(8,128)(2,1)S(1)} %pad_maximum_fusion.own), channel_id=1, source_target_pairs={{0,128},{1,33},{2,130},{3,35},{4,132},{5,37},{6,134},{7,39},{8,136... | collective-permute-start | bytes 3932168 | tf_op jit(solution)/shard_map/ppermute | solution.py:29
  32.6 2.2 %collective-permute-start.8 = (bf16[256,2560]{1,0:T(8,128)(2,1)S(1)}, bf16[256,2560]{1,0:T(8,128)(2,1)}, u32[]{:S(2)}, u32[]{:S(2)}) collective-permute-start(bf16[256,2560]{1,0:T(8,128)(2,1)S(1)} %pad_maximum_fusion.own), channel_id=1, source_target_pairs={{0,386},{1,97},{2,384},{3,99},{4,390},{5,101},{6,388},{7,103},{8,3... | collective-permute-start | bytes 3932168 | tf_op jit(solution)/shard_map/ppermute | solution.py:29
  34.8 3.8 %collective-permute-start.9 = (bf16[256,2560]{1,0:T(8,128)(2,1)S(1)}, bf16[256,2560]{1,0:T(8,128)(2,1)}, u32[]{:S(2)}, u32[]{:S(2)}) collective-permute-start(bf16[256,2560]{1,0:T(8,128)(2,1)S(1)} %pad_maximum_fusion.own), channel_id=1, source_target_pairs={{0,256},{1,65},{2,258},{3,67},{4,260},{5,69},{6,262},{7,71},{8,264... | collective-permute-start | bytes 3932168 | tf_op jit(solution)/shard_map/ppermute | solution.py:29
  38.5 0.0 copy-done
  38.6 1.4 %shard_map.86.filled = f32[6144,128]{1,0:T(8,128)S(1)} custom-call(s32[4]{0:T(128)S(1)} %compare_select_fusion.1.where, bf16[100,4096]{1,0:T(8,128)(2,1)S(1)} %bitcast.7), custom_call_target="tpu_custom_call" | custom-call | flops 2000000000 | bytes 1048576 | tf_op jit(solution)/shard_map/pallas_call | solution.py:279
  39.9 0.0 collective-permute-done.near
  39.9 0.0 collective-permute-done.1.mate
  39.9 0.0 copy-done.2
  39.9 0.0 copy-done.3
  40.0 4.2 %shard_map.87 = (bf16[256,128]{1,0:T(8,128)(2,1)S(1)}, f32[6144,128]{1,0:T(8,128)S(1)}) custom-call(s32[4]{0:T(128)S(1)} %compare_select_fusion.1.where, s32[32,128]{1,0:T(8,128)S(1)} %copy-done.3, bf16[32,16,128]{2,1,0:T(8,128)(2,1)S(1)} %copy-done.2, bf16[100,1024]{1,0:T(8,128)(2,1)} %collective-permute-done.near, ...), custom_call_target="tpu_custom_call", output_to_operand_aliasing={{1}: (5, {})} | custom-call | flops 3000000000 | bytes 1048576 | tf_op jit(solution)/shard_map/pallas_call | solution.py:284
  44.2 3.2 %collective-permute-start.2 = (bf16[256,128]{1,0:T(8,128)(2,1)S(1)}, bf16[256,128]{1,0:T(8,128)(2,1)S(1)}, u32[]{:S(2)}, u32[]{:S(2)}) collective-permute-start(bf16[256,128]{1,0:T(8,128)(2,1)S(1)} %get-tuple-element.14.edge), channel_id=1, source_target_pairs={{0,31},{1,2},{2,1},{3,4},{4,3},{5,6},{6,5},{7,8},{8,7},{9,10},{10,... | collective-permute-start | bytes 196616 | tf_op jit(solution)/shard_map/ppermute | solution.py:52
  47.4 0.0 copy-start.1
  47.4 0.0 copy-start.4
  47.4 3.7 %shard_map.88.inner = bf16[256,128]{1,0:T(8,128)(2,1)S(1)} custom-call(s32[4]{0:T(128)S(1)} %compare_select_fusion.1.where, s32[32,128]{1,0:T(8,128)S(1)} %copy-done.3, bf16[32,16,128]{2,1,0:T(8,128)(2,1)S(1)} %copy-done.2, f32[6144,128]{1,0:T(8,128)S(1)} %get-tuple-element.15.table), custom_call_target="tpu_custom_call" | custom-call | flops 3000000000 | bytes 1048576 | tf_op jit(solution)/shard_map/pallas_call | solution.py:288
  51.1 18.2 %collective-permute-done.2.near = bf16[256,128]{1,0:T(8,128)(2,1)S(1)} collective-permute-done((bf16[256,128]{1,0:T(8,128)(2,1)S(1)}, bf16[256,128]{1,0:T(8,128)(2,1)S(1)}, u32[]{:S(2)}, u32[]{:S(2)}) %collective-permute-start.2) | collective-permute-done | bytes 65568 | tf_op jit(solution)/shard_map/ppermute | solution.py:52
  69.3 1.9 %collective-permute-start.3 = (bf16[768,128]{1,0:T(8,128)(2,1)S(1)}, bf16[768,128]{1,0:T(8,128)(2,1)S(1)}, u32[]{:S(2)}, u32[]{:S(2)}) collective-permute-start(bf16[768,128]{1,0:T(8,128)(2,1)S(1)} %pad_maximum_fusion.2), channel_id=1, source_target_pairs={{0,1},{1,0},{2,3},{3,2},{4,5},{5,4},{6,7},{7,6},{8,9},{9,8},{10,11... | collective-permute-start | bytes 589832 | tf_op jit(solution)/shard_map/ppermute | solution.py:29
  71.3 0.0 copy-done.1
  71.3 0.0 copy-done.4
  71.3 2.3 %shard_map.89 = (bf16[512,1024]{1,0:T(8,128)(2,1)S(1)}, bf16[512,1024]{1,0:T(8,128)(2,1)}) custom-call(s32[4]{0:T(128)S(1)} %compare_select_fusion.1.where, bf16[256,128]{1,0:T(8,128)(2,1)S(1)} %get-tuple-element.14.edge, bf16[256,128]{1,0:T(8,128)(2,1)S(1)} %shard_map.88.inner, bf16[100,1024]{1,0:T(8,128)(2,1)S(1)} %copy-done.1, f32[1,1024]{1,0:T(1,128)S(1)} %bitcast.8), custom_call_target="tpu_custom_call" | custom-call | flops 1500000000 | bytes 1048576 | tf_op jit(solution)/shard_map/pallas_call | solution.py:295
  73.5 0.0 collective-permute-done.3.mate
  73.5 2.0 %shard_map.90.normed = bf16[1024,1024]{1,0:T(8,128)(2,1)S(1)} custom-call(s32[4]{0:T(128)S(1)} %compare_select_fusion.1.where, bf16[256,128]{1,0:T(8,128)(2,1)S(1)} %collective-permute-done.2.near, bf16[768,128]{1,0:T(8,128)(2,1)S(1)} %collective-permute-done.3.mate, bf16[100,1024]{1,0:T(8,128)(2,1)S(1)} %copy-done.1, f32[1,1024]{1,0:T(1,128)S(1)} %bitcast.9), custom_call_target="tpu_custom_call" | custom-call | flops 3000000000 | bytes 1048576 | tf_op jit(solution)/shard_map/pallas_call | solution.py:298
  75.5 0.0 collective-permute-done.7.before
  75.6 0.0 collective-permute-done.8.after
  75.6 0.0 collective-permute-done.9.across
  75.6 4.6 %shard_map.91 = (bf16[4,1024,128]{2,1,0:T(8,128)(2,1)S(1)}, bf16[4,1536,128]{2,1,0:T(8,128)(2,1)S(1)}, bf16[4,1536,128]{2,1,0:T(8,128)(2,1)S(1)}, bf16[1024,1024]{1,0:T(8,128)(2,1)S(1)}, bf16[1024,1536]{1,0:T(8,128)(2,1)S(1)}) custom-call(s32[4]{0:T(128)S(1)} %compare_select_fusion.1.where, bf16[512,1024]{1,0:T(8,128)(2,1)S(1)} %get-tuple-element.17.normed, ...), custom_call_target="tpu_custom_call" | custom-call | flops 3000000000 | bytes 1048576 | tf_op jit(solution)/shard_map/pallas_call | solution.py:302
  80.2 4.6 %shard_map.92 = (bf16[4,1024,128]{2,1,0:T(8,128)(2,1)S(1)}, bf16[4,1536,128]{2,1,0:T(8,128)(2,1)S(1)}, bf16[4,1536,128]{2,1,0:T(8,128)(2,1)S(1)}) custom-call(s32[4]{0:T(128)S(1)} %compare_select_fusion.1.where, bf16[1024,1024]{1,0:T(8,128)(2,1)S(1)} %shard_map.90.normed, ...), custom_call_target="tpu_custom_call", output_to_operand_aliasing={{0}: (3, {}), {1}: (4, {}), {2}: (5, {})} | custom-call | flops 5000000000 | bytes 1048576 | tf_op jit(solution)/shard_map/pallas_call | solution.py:310
  84.8 5.1 %shard_map.94 = bf16[4,512,128]{2,1,0:T(8,128)(2,1)S(1)} custom-call(s32[1]{0:T(128)} %bitcast.4.shard, bf16[4,1024,128]{2,1,0:T(8,128)(2,1)S(1)} %get-tuple-element.22.q, bf16[4,1536,128]{2,1,0:T(8,128)(2,1)S(1)} %get-tuple-element.23.k, bf16[4,1536,128]{2,1,0:T(8,128)(2,1)S(1)} %get-tuple-element.24.v), custom_call_target="tpu_custom_call" | custom-call | flops 8000000000 | bytes 1048576 | tf_op jit(solution)/shard_map/pallas_call | solution.py:314
  89.8 2.4 %collective-permute-start.10 = (bf16[4,512,128]{2,1,0:T(8,128)(2,1)S(1)}, bf16[4,512,128]{2,1,0:T(8,128)(2,1)S(1)}, u32[]{:S(2)}, u32[]{:S(2)}) collective-permute-start(bf16[4,512,128]{2,1,0:T(8,128)(2,1)S(1)} %shard_map.94), channel_id=1, source_target_pairs={{0,1},{1,0},{2,3},{3,2},{4,5},{5,4},{6,7},{7,6},{8,9},{9,8},{10,11... | collective-permute-start | bytes 1572872 | tf_op jit(solution)/shard_map/ppermute | solution.py:29
  92.3 5.1 %shard_map.93.mine = bf16[4,512,128]{2,1,0:T(8,128)(2,1)S(1)} custom-call(s32[1]{0:T(128)} %bitcast.3.shard, bf16[4,1024,128]{2,1,0:T(8,128)(2,1)S(1)} %get-tuple-element.22.q, bf16[4,1536,128]{2,1,0:T(8,128)(2,1)S(1)} %get-tuple-element.23.k, bf16[4,1536,128]{2,1,0:T(8,128)(2,1)S(1)} %get-tuple-element.24.v), custom_call_target="tpu_custom_call" | custom-call | flops 8000000000 | bytes 1048576 | tf_op jit(solution)/shard_map/pallas_call | solution.py:316
  97.4 0.0 collective-permute-done.10.theirs
  97.4 2.8 %shard_map.95 = bf16[512,1024]{1,0:T(8,128)(2,1)} custom-call(s32[4]{0:T(128)S(1)} %compare_select_fusion.1.where, bf16[4,512,128]{2,1,0:T(8,128)(2,1)S(1)} %shard_map.93.mine, bf16[4,512,128]{2,1,0:T(8,128)(2,1)S(1)} %collective-permute-done.10.theirs, bf16[1024,1024]{1,0:T(8,128)(2,1)S(1)} %get-tuple-element.25.rows), custom_call_target="tpu_custom_call" | custom-call | flops 1000000000 | bytes 1048576 | tf_op jit(solution)/shard_map/pallas_call | solution.py:317
  (2 shorter events, 0.0 us)
Async XLA Ops:
  0.6 28.6 %copy-start.5 = (bf16[64,1024]{1,0:T(8,128)(2,1)S(1)}, bf16[64,1024]{1,0:T(8,128)(2,1)}, u32[]{:S(2)}) copy-start(bf16[64,1024]{1,0:T(8,128)(2,1)} %param.13) | copy-start | bytes 393220
  1.7 36.8 %copy-start = (bf16[1,100,4096]{2,1,0:T(8,128)(2,1)S(1)}, bf16[1,100,4096]{2,1,0:T(8,128)(2,1)}, u32[]{:S(2)}) copy-start(bf16[1,100,4096]{2,1,0:T(8,128)(2,1)} %param.7) | copy-start | bytes 2457604
  2.7 26.5 %collective-permute-start.4 = (bf16[64,2560]{1,0:T(8,128)(2,1)S(1)}, bf16[64,2560]{1,0:T(8,128)(2,1)S(1)}, u32[]{:S(2)}, u32[]{:S(2)}) collective-permute-start(bf16[64,2560]{1,0:T(8,128)(2,1)S(1)} %pad_maximum_fusion.1), channel_id=1, source_target_pairs={{0,32},{1,129},{2,34},{3,131},{4,36},{5,133},{6,38},{7,135},{8,40}... | collective-permute-start | bytes 983048 | tf_op jit(solution)/shard_map/ppermute | solution.py:29
  7.2 22.0 %collective-permute-start.5 = (bf16[64,2560]{1,0:T(8,128)(2,1)S(1)}, bf16[64,2560]{1,0:T(8,128)(2,1)S(1)}, u32[]{:S(2)}, u32[]{:S(2)}) collective-permute-start(bf16[64,2560]{1,0:T(8,128)(2,1)S(1)} %pad_maximum_fusion.1), channel_id=1, source_target_pairs={{0,96},{1,387},{2,98},{3,385},{4,100},{5,391},{6,102},{7,389},{8,1... | collective-permute-start | bytes 983048 | tf_op jit(solution)/shard_map/ppermute | solution.py:29
  9.1 20.1 %collective-permute-start.6 = (bf16[64,2560]{1,0:T(8,128)(2,1)S(1)}, bf16[64,2560]{1,0:T(8,128)(2,1)S(1)}, u32[]{:S(2)}, u32[]{:S(2)}) collective-permute-start(bf16[64,2560]{1,0:T(8,128)(2,1)S(1)} %pad_maximum_fusion.1), channel_id=1, source_target_pairs={{0,64},{1,257},{2,66},{3,259},{4,68},{5,261},{6,70},{7,263},{8,72}... | collective-permute-start | bytes 983048 | tf_op jit(solution)/shard_map/ppermute | solution.py:29
  12.8 27.1 %collective-permute-start = (bf16[100,1024]{1,0:T(8,128)(2,1)}, bf16[100,1024]{1,0:T(8,128)(2,1)}, u32[]{:S(2)}, u32[]{:S(2)}) collective-permute-start(bf16[100,1024]{1,0:T(8,128)(2,1)} %get-tuple-element.27), channel_id=1, source_target_pairs={{0,31},{1,2},{2,1},{3,4},{4,3},{5,6},{6,5},{7,8},{8,7},{9,10},{10,... | collective-permute-start | bytes 614408 | tf_op jit(solution)/shard_map/ppermute | solution.py:52
  19.8 20.2 %collective-permute-start.1 = (bf16[100,1024]{1,0:T(8,128)(2,1)}, bf16[100,1024]{1,0:T(8,128)(2,1)}, u32[]{:S(2)}, u32[]{:S(2)}) collective-permute-start(bf16[100,1024]{1,0:T(8,128)(2,1)} %get-tuple-element.26), channel_id=1, source_target_pairs={{0,1},{1,0},{2,3},{3,2},{4,5},{5,4},{6,7},{7,6},{8,9},{9,8},{10,11... | collective-permute-start | bytes 614408 | tf_op jit(solution)/shard_map/ppermute | solution.py:29
  29.3 10.6 %copy-start.2 = (bf16[32,16,128]{2,1,0:T(8,128)(2,1)S(1)}, bf16[32,16,128]{2,1,0:T(8,128)(2,1)}, u32[]{:S(2)}) copy-start(bf16[32,16,128]{2,1,0:T(8,128)(2,1)} %weight.3) | copy-start | bytes 393220
  29.3 10.6 %copy-start.3 = (s32[32,128]{1,0:T(8,128)S(1)}, s32[32,128]{1,0:T(8,128)}, u32[]{:S(2)}) copy-start(s32[32,128]{1,0:T(8,128)} %index.3) | copy-start | bytes 49156
  29.3 46.2 %collective-permute-start.7 = (bf16[256,2560]{1,0:T(8,128)(2,1)S(1)}, bf16[256,2560]{1,0:T(8,128)(2,1)S(1)}, u32[]{:S(2)}, u32[]{:S(2)}) collective-permute-start(bf16[256,2560]{1,0:T(8,128)(2,1)S(1)} %pad_maximum_fusion.own), channel_id=1, source_target_pairs={{0,128},{1,33},{2,130},{3,35},{4,132},{5,37},{6,134},{7,39},{8,136... | collective-permute-start | bytes 3932168 | tf_op jit(solution)/shard_map/ppermute | solution.py:29
  32.6 42.9 %collective-permute-start.8 = (bf16[256,2560]{1,0:T(8,128)(2,1)S(1)}, bf16[256,2560]{1,0:T(8,128)(2,1)}, u32[]{:S(2)}, u32[]{:S(2)}) collective-permute-start(bf16[256,2560]{1,0:T(8,128)(2,1)S(1)} %pad_maximum_fusion.own), channel_id=1, source_target_pairs={{0,386},{1,97},{2,384},{3,99},{4,390},{5,101},{6,388},{7,103},{8,3... | collective-permute-start | bytes 3932168 | tf_op jit(solution)/shard_map/ppermute | solution.py:29
  34.8 40.8 %collective-permute-start.9 = (bf16[256,2560]{1,0:T(8,128)(2,1)S(1)}, bf16[256,2560]{1,0:T(8,128)(2,1)}, u32[]{:S(2)}, u32[]{:S(2)}) collective-permute-start(bf16[256,2560]{1,0:T(8,128)(2,1)S(1)} %pad_maximum_fusion.own), channel_id=1, source_target_pairs={{0,256},{1,65},{2,258},{3,67},{4,260},{5,69},{6,262},{7,71},{8,264... | collective-permute-start | bytes 3932168 | tf_op jit(solution)/shard_map/ppermute | solution.py:29
  44.2 25.2 %collective-permute-start.2 = (bf16[256,128]{1,0:T(8,128)(2,1)S(1)}, bf16[256,128]{1,0:T(8,128)(2,1)S(1)}, u32[]{:S(2)}, u32[]{:S(2)}) collective-permute-start(bf16[256,128]{1,0:T(8,128)(2,1)S(1)} %get-tuple-element.14.edge), channel_id=1, source_target_pairs={{0,31},{1,2},{2,1},{3,4},{4,3},{5,6},{6,5},{7,8},{8,7},{9,10},{10,... | collective-permute-start | bytes 196616 | tf_op jit(solution)/shard_map/ppermute | solution.py:52
  47.4 23.9 %copy-start.1 = (bf16[100,1024]{1,0:T(8,128)(2,1)S(1)}, bf16[100,1024]{1,0:T(8,128)(2,1)}, u32[]{:S(2)}) copy-start(bf16[100,1024]{1,0:T(8,128)(2,1)} %w_in.3) | copy-start | bytes 614404
  47.4 23.9 %copy-start.4 = (f32[1024]{0:T(1024)S(1)}, f32[1024]{0:T(1024)}, u32[]{:S(2)}) copy-start(f32[1024]{0:T(1024)} %param.11) | copy-start | bytes 12292
  69.3 4.2 %collective-permute-start.3 = (bf16[768,128]{1,0:T(8,128)(2,1)S(1)}, bf16[768,128]{1,0:T(8,128)(2,1)S(1)}, u32[]{:S(2)}, u32[]{:S(2)}) collective-permute-start(bf16[768,128]{1,0:T(8,128)(2,1)S(1)} %pad_maximum_fusion.2), channel_id=1, source_target_pairs={{0,1},{1,0},{2,3},{3,2},{4,5},{5,4},{6,7},{7,6},{8,9},{9,8},{10,11... | collective-permute-start | bytes 589832 | tf_op jit(solution)/shard_map/ppermute | solution.py:29
  89.8 7.5 %collective-permute-start.10 = (bf16[4,512,128]{2,1,0:T(8,128)(2,1)S(1)}, bf16[4,512,128]{2,1,0:T(8,128)(2,1)S(1)}, u32[]{:S(2)}, u32[]{:S(2)}) collective-permute-start(bf16[4,512,128]{2,1,0:T(8,128)(2,1)S(1)} %shard_map.94), channel_id=1, source_target_pairs={{0,1},{1,0},{2,3},{3,2},{4,5},{5,4},{6,7},{7,6},{8,9},{9,8},{10,11... | collective-permute-start | bytes 1572872 | tf_op jit(solution)/shard_map/ppermute | solution.py:29
where the time goes:
time: 101 us; the launch traced here: 100 us
  starting transfers between devices  41.3 us (41%)
  Pallas kernels  35.6 us (35%)
  waiting for transfers between devices  18.2 us (18%)
  other arithmetic  3.99 us (4%)
    ppermute x9, starting transfers between devices, send(): return lax.ppermute(array, AXES, pairs)  31.2 us
    ppermute x2, waiting for transfers between devices, ring(): return lax.ppermute(array, 'space', [(s, move(s) % 32) for s in range(32)])  18.2 us
    ppermute x2, starting transfers between devices, ring(): return lax.ppermute(array, 'space', [(s, move(s) % 32) for s in range(32)])  10.1 us
    pallas_call x1, Pallas kernels, shards(): mine, = attend(core[None], q, k, v)  5.06 us
    pallas_call x1, Pallas kernels, shards(): other, = attend((1 - core)[None], q, k, v)  5.06 us
    pallas_call x1, Pallas kernels, shards(): call(project_own_kernel, shapes + [((1024, 1024), BF), ((1024, 1536), BF)...  4.6 us
    pallas_call x1, Pallas kernels, shards(): call(project_rest_kernel, shapes, [], 5000000000, 12, 5, {3: 0, 4: 1, 5: 2})  4.59 us
    pallas_call x1, Pallas kernels, shards(): call(encode_edge_kernel, [part, grown], [tall, picked], 3000000000, 8, 4,...  4.2 us
  transfers between devices with their start and end apart: 11, of which 1 were waited for; matrix products, arithmetic and copies ran while one was open for 2% of the time, Pallas kernels for 19%

commit v1 on v0

--- a/solution.py
+++ b/solution.py
@@ -184,33 +184,35 @@
         unit_heads(dot(rows, weights[:, :512]), ones, q, q_at)
 
 
-def project_own_kernel(where, normed, own, before, after, across, q, k, v, out_rows, weights):
+def place(where, step, piece, weights, out_cols):
     core, x, y = where[0], where[1], where[2]
     first, second = jnp.where(core == 0, x, y), jnp.where(core == 0, y, x)
-    for step, piece in zip(SOURCES, (own, before, after, across)):
-        other = lax.rem(second + step, 4)
-        for m in range(4):
-            mine = lax.rem(first + SOURCES[m], 4)
-            block = jnp.where(core == 0, other * 4 + mine, mine * 4 + other)
-            rows = pl.ds(pl.multiple_of(block * 64, 64), 64)
-            weights[rows, :] = piece[m * 64 : (m + 1) * 64, :1536]
-            out_rows[rows, :] = piece[m * 64 : (m + 1) * 64, 1536:]
+    other = lax.rem(second + step, 4)
+    for m in range(4):
+        mine = lax.rem(first + SOURCES[m], 4)
+        block = jnp.where(core == 0, other * 4 + mine, mine * 4 + other)
+        rows = pl.ds(pl.multiple_of(block * 64, 64), 64)
+        weights[rows, :] = piece[m * 64 : (m + 1) * 64, :1536]
+        out_cols[rows, :] = piece[m * 64 : (m + 1) * 64, 1536:]
+
+
+def assemble_kernel(where, own, before, after, weights, out_cols):
+    for step, piece in zip(SOURCES, (own, before, after)):
+        place(where, step, piece, weights, out_cols)
+
+
+def project_kernel(
+    where, own, rest, across, most, most_cols, q, k, v, weights, out_cols
+):
+    core = where[0]
+    place(where, SOURCES[3], across, weights, out_cols)
     ones = head_ones()
-    start = core * 512
-    for i in range(0, 512, 256):
-        rows = normed[i : i + 256, :]
-        project_tile(rows, weights, ones, q, k, v, rows_at(start + i), rows_at(start + i + 256))
-
-
-def project_rest_kernel(where, normed, weights, q_in, k_in, v_in, q, k, v):
-    core = where[0]
-    ones = head_ones()
-    start = 512 - core * 512
-    for i in range(0, 512, 256):
-        rows = normed[i : i + 256, :]
-        project_tile(rows, weights, ones, q, k, v, rows_at(start + i), rows_at(start + i + 256))
+    for rows, start in ((own, core * 512), (rest, 512 - core * 512)):
+        for i in range(0, 512, 256):
+            at = rows_at(start + i), rows_at(start + i + 256)
+            project_tile(rows[i : i + 256, :], weights, ones, q, k, v, *at)
     for i, at in ((512, 1280 - core * 1280), (768, core * 1280)):
-        project_tile(normed[i : i + 256, :], weights, ones, q, k, v, None, rows_at(at))
+        project_tile(rest[i : i + 256, :], weights, ones, q, k, v, None, rows_at(at))
 
 
 def attend_kernel(shard, q, k, v, out):
@@ -241,12 +243,14 @@
     lax.fori_loop(0, 4, tile, 0)
 
 
-def out_kernel(where, mine, theirs, rows, update):
+def out_kernel(where, mine, theirs, my_cols, their_cols, update):
     core = where[0]
     join = lambda ref: jnp.concatenate([ref[p] for p in range(4)], axis=1)
-    near = rows[pl.ds(pl.multiple_of(core * 512, 512), 512), :]
-    far = rows[pl.ds(pl.multiple_of(512 - core * 512, 512), 512), :]
-    update[...] = (dot(join(mine), near) + dot(join(theirs), far)).astype(BF)
+    here, there = join(mine), join(theirs)
+    near = pl.ds(pl.multiple_of(core * 512, 512), 512)
+    far = pl.ds(pl.multiple_of(512 - core * 512, 512), 512)
+    for cols, at in ((my_cols, near), (their_cols, far)):
+        update[:, at] = (dot(here, cols[near, :]) + dot(there, cols[far, :])).astype(BF)
 
 
 def shards(fields, cell_index, interp_weight, w_in, ln_gain, w_qkv, w_out):
@@ -263,9 +267,9 @@
 
     halves = [
         jnp.where(even, w[:, i : i + 512], w[:, i + 512 : i + 1024])
-        for w, i in ((w_qkv, 0), (w_qkv, 1024), (w_qkv, 2048))
+        for w, i in ((w_qkv, 0), (w_qkv, 1024), (w_qkv, 2048), (w_out, 0))
     ]
-    block = jnp.concatenate(halves + [w_out], axis=1)
+    block = jnp.concatenate(halves, axis=1)
     line = [block]
     for shift in STEPS:
         line.append(send(block, along(True, shift)))
@@ -298,24 +302,19 @@
     (rest_normed,) = call(
         embed_rest_kernel, [((1024, 1024), BF)], wide, 3_000_000_000, 12, 4
     )(where, near, mate, w_in, gain)
+    grand = [((1024, 1536), BF), ((1024, 512), BF)]
+    most = call(assemble_kernel, grand, [], 500_000_000, 8, 3)(where, *gathered[:3])
     shapes = [((4, 1024, 128), BF), ((4, 1536, 128), BF), ((4, 1536, 128), BF)]
-    q, k, v, out_rows, weights = call(
-        project_own_kernel,
-        shapes + [((1024, 1024), BF), ((1024, 1536), BF)],
-        [],
-        3_000_000_000,
-        12,
-        5,
-    )(where, own_normed, *gathered)
-    q, k, v = call(
-        project_rest_kernel, shapes, [], 5_000_000_000, 12, 5, {3: 0, 4: 1, 5: 2}
-    )(where, rest_normed, weights, q, k, v)
+    q, k, v, _, my_cols = call(
+        project_kernel, shapes + grand, [], 8_000_000_000, 12, 5, {4: 3, 5: 4}
+    )(where, own_normed, rest_normed, gathered[3], *most)
+    their_cols = swap(my_cols)
     attend = call(attend_kernel, [((4, 512, 128), BF)], [], 8_000_000_000, 16, 3)
     (other,) = attend((1 - core)[None], q, k, v)
     theirs = swap(other)
     (mine,) = attend(core[None], q, k, v)
-    (update,) = call(out_kernel, [((512, 1024), BF)], [], 1_000_000_000, 8, 3)(
-        where, mine, theirs, out_rows
+    (update,) = call(out_kernel, [((512, 1024), BF)], [], 1_000_000_000, 8, 4)(
+        where, mine, theirs, my_cols, their_cols
     )
     return latent[None], update[None]
 

time: 101 us -> 99.5 us (0.985)
  the two profiles are of different devices: /device:TPU:27 before, /device:TPU:11 now
where the time goes in v1:
time: 99.5 us; the launch traced here: 98.9 us
  starting transfers between devices  47.5 us (48%)
  Pallas kernels  34.9 us (35%)
  waiting for transfers between devices  10.8 us (11%)
  other arithmetic  3.82 us (4%)
    ppermute x10, starting transfers between devices, send(): return lax.ppermute(array, AXES, pairs)  34.3 us
    ppermute x2, starting transfers between devices, ring(): return lax.ppermute(array, 'space', [(s, move(s) % 32) for s in range(32)])  13.1 us
    ppermute x2, waiting for transfers between devices, ring(): return lax.ppermute(array, 'space', [(s, move(s) % 32) for s in range(32)])  10.8 us
    pallas_call x1, Pallas kernels, shards(): call(project_kernel, shapes + grand, [], 8000000000, 12, 5, {4: 3, 5: 4})  7.76 us
    pallas_call x1, Pallas kernels, shards(): mine, = attend(core[None], q, k, v)  5.06 us
    pallas_call x1, Pallas kernels, shards(): other, = attend((1 - core)[None], q, k, v)  5.06 us
    pallas_call x1, Pallas kernels, shards(): call(encode_edge_kernel, [part, grown], [tall, picked], 3000000000, 8, 4,...  4.2 us
    pallas_call x1, Pallas kernels, shards(): call(encode_inner_kernel, [part], [picked], 3000000000, 8, 2, {}, 2)  3.75 us
  transfers between devices with their start and end apart: 12, of which 1 were waited for; matrix products, arithmetic and copies ran while one was open for 3% of the time, Pallas kernels for 25%

profile of v1, /device:TPU:11, one launch (start us, length us, event | category | flops | bytes accessed | tf_op | source)
XLA Modules:
  0.0 98.9 jit_solution(16007077228523195564)
XLA Ops:
  0.6 0.0 copy-start
  0.7 1.2 %slice_select_fusion.3 = (bf16[64,512]{1,0:T(8,128)(2,1)S(1)}, bf16[64,512]{1,0:T(8,128)(2,1)S(1)}, bf16[64,512]{1,0:T(8,128)(2,1)S(1)}, bf16[64,512]{1,0:T(8,128)(2,1)S(1)}) fusion(bf16[64,3072]{1,0:T(8,128)(2,1)} %param.12, pred[]{:T(512)S(6)} %eq.11, bf16[64,1024]{1,0:T(8,128)(2,1)} %param.13), kind=kLoop, calls=%fused_computation.8 | loop fusion | flops 131072 | bytes 786433 | tf_op jit(solution)/shard_map/jit(_where)/select_n | solution.py:269
  1.9 5.0 %collective-permute-start.6 = (bf16[64,2048]{1,0:T(8,128)(2,1)S(1)}, bf16[64,2048]{1,0:T(8,128)(2,1)S(1)}, u32[]{:S(2)}, u32[]{:S(2)}) collective-permute-start(bf16[64,2048]{1,0:T(8,128)(2,1)S(1)} %pad_maximum_fusion.1), channel_id=1, source_target_pairs={{0,64},{1,257},{2,66},{3,259},{4,68},{5,261},{6,70},{7,263},{8,72}... | collective-permute-start | bytes 786440 | tf_op jit(solution)/shard_map/ppermute | solution.py:29
  6.8 1.9 %collective-permute-start.5 = (bf16[64,2048]{1,0:T(8,128)(2,1)S(1)}, bf16[64,2048]{1,0:T(8,128)(2,1)S(1)}, u32[]{:S(2)}, u32[]{:S(2)}) collective-permute-start(bf16[64,2048]{1,0:T(8,128)(2,1)S(1)} %pad_maximum_fusion.1), channel_id=1, source_target_pairs={{0,96},{1,387},{2,98},{3,385},{4,100},{5,391},{6,102},{7,389},{8,1... | collective-permute-start | bytes 786440 | tf_op jit(solution)/shard_map/ppermute | solution.py:29
  8.8 3.6 %collective-permute-start.4 = (bf16[64,2048]{1,0:T(8,128)(2,1)S(1)}, bf16[64,2048]{1,0:T(8,128)(2,1)S(1)}, u32[]{:S(2)}, u32[]{:S(2)}) collective-permute-start(bf16[64,2048]{1,0:T(8,128)(2,1)S(1)} %pad_maximum_fusion.1), channel_id=1, source_target_pairs={{0,32},{1,129},{2,34},{3,131},{4,36},{5,133},{6,38},{7,135},{8,40}... | collective-permute-start | bytes 786440 | tf_op jit(solution)/shard_map/ppermute | solution.py:29
  12.4 1.8 %broadcast_select_fusion = (bf16[100,1024]{1,0:T(8,128)(2,1)}, bf16[100,1024]{1,0:T(8,128)(2,1)}) fusion(pred[]{:T(512)S(6)} %eq.11, bf16[100,4096]{1,0:T(8,128)(2,1)} %bitcast.6), kind=kLoop, calls=%fused_computation.2 | loop fusion | flops 204800 | bytes 819201 | tf_op jit(solution)/shard_map/jit(_where)/select_n | solution.py:266
  14.3 6.4 %collective-permute-start = (bf16[100,1024]{1,0:T(8,128)(2,1)}, bf16[100,1024]{1,0:T(8,128)(2,1)}, u32[]{:S(2)}, u32[]{:S(2)}) collective-permute-start(bf16[100,1024]{1,0:T(8,128)(2,1)} %get-tuple-element.23), channel_id=1, source_target_pairs={{0,31},{1,2},{2,1},{3,4},{4,3},{5,6},{6,5},{7,8},{8,7},{9,10},{10,... | collective-permute-start | bytes 614408 | tf_op jit(solution)/shard_map/ppermute | solution.py:52
  20.7 8.5 %collective-permute-start.1 = (bf16[100,1024]{1,0:T(8,128)(2,1)}, bf16[100,1024]{1,0:T(8,128)(2,1)}, u32[]{:S(2)}, u32[]{:S(2)}) collective-permute-start(bf16[100,1024]{1,0:T(8,128)(2,1)} %get-tuple-element.22), channel_id=1, source_target_pairs={{0,1},{1,0},{2,3},{3,2},{4,5},{5,4},{6,7},{7,6},{8,9},{9,8},{10,11... | collective-permute-start | bytes 614408 | tf_op jit(solution)/shard_map/ppermute | solution.py:29
  29.2 0.0 copy-done
  29.2 0.0 copy-start.2
  29.2 0.0 copy-start.3
  29.2 1.4 %shard_map.86.filled = f32[6144,128]{1,0:T(8,128)S(1)} custom-call(s32[4]{0:T(128)S(1)} %compare_select_fusion.1.where, bf16[100,4096]{1,0:T(8,128)(2,1)S(1)} %bitcast.7), custom_call_target="tpu_custom_call" | custom-call | flops 2000000000 | bytes 1048576 | tf_op jit(solution)/shard_map/pallas_call | solution.py:283
  30.6 0.0 collective-permute-done.6
  30.6 0.0 collective-permute-done.5
  30.6 0.0 collective-permute-done.4
  30.6 0.1 pad_maximum_fusion.own
  30.7 3.8 %collective-permute-start.7 = (bf16[256,2048]{1,0:T(8,128)(2,1)S(1)}, bf16[256,2048]{1,0:T(8,128)(2,1)}, u32[]{:S(2)}, u32[]{:S(2)}) collective-permute-start(bf16[256,2048]{1,0:T(8,128)(2,1)S(1)} %pad_maximum_fusion.own), channel_id=1, source_target_pairs={{0,256},{1,65},{2,258},{3,67},{4,260},{5,69},{6,262},{7,71},{8,264... | collective-permute-start | bytes 3145736 | tf_op jit(solution)/shard_map/ppermute | solution.py:29
  34.5 1.9 %collective-permute-start.8 = (bf16[256,2048]{1,0:T(8,128)(2,1)S(1)}, bf16[256,2048]{1,0:T(8,128)(2,1)S(1)}, u32[]{:S(2)}, u32[]{:S(2)}) collective-permute-start(bf16[256,2048]{1,0:T(8,128)(2,1)S(1)} %pad_maximum_fusion.own), channel_id=1, source_target_pairs={{0,128},{1,33},{2,130},{3,35},{4,132},{5,37},{6,134},{7,39},{8,136... | collective-permute-start | bytes 3145736 | tf_op jit(solution)/shard_map/ppermute | solution.py:29
  36.4 3.4 %collective-permute-start.9 = (bf16[256,2048]{1,0:T(8,128)(2,1)S(1)}, bf16[256,2048]{1,0:T(8,128)(2,1)S(1)}, u32[]{:S(2)}, u32[]{:S(2)}) collective-permute-start(bf16[256,2048]{1,0:T(8,128)(2,1)S(1)} %pad_maximum_fusion.own), channel_id=1, source_target_pairs={{0,386},{1,97},{2,384},{3,99},{4,390},{5,101},{6,388},{7,103},{8,3... | collective-permute-start | bytes 3145736 | tf_op jit(solution)/shard_map/ppermute | solution.py:29
  39.8 0.0 collective-permute-done.near
  39.8 0.0 collective-permute-done.1.mate
  39.8 0.0 copy-done.2
  39.8 0.0 copy-done.3
  39.8 4.2 %shard_map.87 = (bf16[256,128]{1,0:T(8,128)(2,1)S(1)}, f32[6144,128]{1,0:T(8,128)S(1)}) custom-call(s32[4]{0:T(128)S(1)} %compare_select_fusion.1.where, s32[32,128]{1,0:T(8,128)S(1)} %copy-done.3, bf16[32,16,128]{2,1,0:T(8,128)(2,1)S(1)} %copy-done.2, bf16[100,1024]{1,0:T(8,128)(2,1)} %collective-permute-done.near, ...), custom_call_target="tpu_custom_call", output_to_operand_aliasing={{1}: (5, {})} | custom-call | flops 3000000000 | bytes 1048576 | tf_op jit(solution)/shard_map/pallas_call | solution.py:288
  44.1 6.7 %collective-permute-start.2 = (bf16[256,128]{1,0:T(8,128)(2,1)S(1)}, bf16[256,128]{1,0:T(8,128)(2,1)S(1)}, u32[]{:S(2)}, u32[]{:S(2)}) collective-permute-start(bf16[256,128]{1,0:T(8,128)(2,1)S(1)} %get-tuple-element.12.edge), channel_id=1, source_target_pairs={{0,31},{1,2},{2,1},{3,4},{4,3},{5,6},{6,5},{7,8},{8,7},{9,10},{10,... | collective-permute-start | bytes 196616 | tf_op jit(solution)/shard_map/ppermute | solution.py:52
  50.8 0.0 copy-start.4
  50.8 3.7 %shard_map.88.inner = bf16[256,128]{1,0:T(8,128)(2,1)S(1)} custom-call(s32[4]{0:T(128)S(1)} %compare_select_fusion.1.where, s32[32,128]{1,0:T(8,128)S(1)} %copy-done.3, bf16[32,16,128]{2,1,0:T(8,128)(2,1)S(1)} %copy-done.2, f32[6144,128]{1,0:T(8,128)S(1)} %get-tuple-element.13.table), custom_call_target="tpu_custom_call" | custom-call | flops 3000000000 | bytes 1048576 | tf_op jit(solution)/shard_map/pallas_call | solution.py:292
  54.5 10.8 %collective-permute-done.2.near = bf16[256,128]{1,0:T(8,128)(2,1)S(1)} collective-permute-done((bf16[256,128]{1,0:T(8,128)(2,1)S(1)}, bf16[256,128]{1,0:T(8,128)(2,1)S(1)}, u32[]{:S(2)}, u32[]{:S(2)}) %collective-permute-start.2) | collective-permute-done | bytes 65568 | tf_op jit(solution)/shard_map/ppermute | solution.py:52
  65.3 0.7 pad_maximum_fusion.2
  66.0 1.9 %collective-permute-start.3 = (bf16[768,128]{1,0:T(8,128)(2,1)}, bf16[768,128]{1,0:T(8,128)(2,1)S(1)}, u32[]{:S(2)}, u32[]{:S(2)}) collective-permute-start(bf16[768,128]{1,0:T(8,128)(2,1)} %pad_maximum_fusion.2), channel_id=1, source_target_pairs={{0,1},{1,0},{2,3},{3,2},{4,5},{5,4},{6,7},{7,6},{8,9},{9,8},{10,11... | collective-permute-start | bytes 589832 | tf_op jit(solution)/shard_map/ppermute | solution.py:29
  67.9 0.0 copy-done.4
  67.9 0.0 copy-start.1
  67.9 0.9 copy-done.1
  68.9 2.3 %shard_map.89 = (bf16[512,1024]{1,0:T(8,128)(2,1)S(1)}, bf16[512,1024]{1,0:T(8,128)(2,1)}) custom-call(s32[4]{0:T(128)S(1)} %compare_select_fusion.1.where, bf16[256,128]{1,0:T(8,128)(2,1)S(1)} %get-tuple-element.12.edge, bf16[256,128]{1,0:T(8,128)(2,1)S(1)} %shard_map.88.inner, bf16[100,1024]{1,0:T(8,128)(2,1)S(1)} %copy-done.1, f32[1,1024]{1,0:T(1,128)S(1)} %bitcast.8), custom_call_target="tpu_custom_call" | custom-call | flops 1500000000 | bytes 1048576 | tf_op jit(solution)/shard_map/pallas_call | solution.py:299
  71.1 0.0 collective-permute-done.3.mate
  71.1 2.0 %shard_map.90.rest = bf16[1024,1024]{1,0:T(8,128)(2,1)S(1)} custom-call(s32[4]{0:T(128)S(1)} %compare_select_fusion.1.where, bf16[256,128]{1,0:T(8,128)(2,1)S(1)} %collective-permute-done.2.near, bf16[768,128]{1,0:T(8,128)(2,1)S(1)} %collective-permute-done.3.mate, bf16[100,1024]{1,0:T(8,128)(2,1)S(1)} %copy-done.1, f32[1,1024]{1,0:T(1,128)S(1)} %bitcast.9), custom_call_target="tpu_custom_call" | custom-call | flops 3000000000 | bytes 1048576 | tf_op jit(solution)/shard_map/pallas_call | solution.py:302
  73.1 0.0 collective-permute-done.8.before
  73.1 0.0 collective-permute-done.9.after
  73.1 0.8 shard_map.91
  73.9 0.0 collective-permute-done.7.across
  73.9 7.8 %shard_map.92 = (bf16[4,1024,128]{2,1,0:T(8,128)(2,1)S(1)}, bf16[4,1536,128]{2,1,0:T(8,128)(2,1)S(1)}, bf16[4,1536,128]{2,1,0:T(8,128)(2,1)S(1)}, bf16[1024,1536]{1,0:T(8,128)(2,1)S(1)}, bf16[1024,512]{1,0:T(8,128)(2,1)S(1)}) custom-call(s32[4]{0:T(128)S(1)} %compare_select_fusion.1.where, ...), custom_call_target="tpu_custom_call", output_to_operand_aliasing={{3}: (4, {}), {4}: (5, {})} | custom-call | flops 8000000000 | bytes 1048576 | tf_op jit(solution)/shard_map/pallas_call | solution.py:308
  81.7 2.4 %collective-permute-start.11 = (bf16[1024,512]{1,0:T(8,128)(2,1)S(1)}, bf16[1024,512]{1,0:T(8,128)(2,1)S(1)}, u32[]{:S(2)}, u32[]{:S(2)}) collective-permute-start(bf16[1024,512]{1,0:T(8,128)(2,1)S(1)} %get-tuple-element.21.my_cols), channel_id=1, source_target_pairs={{0,1},{1,0},{2,3},{3,2},{4,5},{5,4},{6,7},{7,6},{8,9},{9,8},{10,11... | collective-permute-start | bytes 3145736 | tf_op jit(solution)/shard_map/ppermute | solution.py:29
  84.1 5.1 %shard_map.94 = bf16[4,512,128]{2,1,0:T(8,128)(2,1)S(1)} custom-call(s32[1]{0:T(128)} %bitcast.4.shard, bf16[4,1024,128]{2,1,0:T(8,128)(2,1)S(1)} %get-tuple-element.18.q, bf16[4,1536,128]{2,1,0:T(8,128)(2,1)S(1)} %get-tuple-element.19.k, bf16[4,1536,128]{2,1,0:T(8,128)(2,1)S(1)} %get-tuple-element.20.v), custom_call_target="tpu_custom_call" | custom-call | flops 8000000000 | bytes 1048576 | tf_op jit(solution)/shard_map/pallas_call | solution.py:313
  89.2 1.9 %collective-permute-start.10 = (bf16[4,512,128]{2,1,0:T(8,128)(2,1)S(1)}, bf16[4,512,128]{2,1,0:T(8,128)(2,1)S(1)}, u32[]{:S(2)}, u32[]{:S(2)}) collective-permute-start(bf16[4,512,128]{2,1,0:T(8,128)(2,1)S(1)} %shard_map.94), channel_id=1, source_target_pairs={{0,1},{1,0},{2,3},{3,2},{4,5},{5,4},{6,7},{7,6},{8,9},{9,8},{10,11... | collective-permute-start | bytes 1572872 | tf_op jit(solution)/shard_map/ppermute | solution.py:29
  91.1 5.1 %shard_map.93.mine = bf16[4,512,128]{2,1,0:T(8,128)(2,1)S(1)} custom-call(s32[1]{0:T(128)} %bitcast.3.shard, bf16[4,1024,128]{2,1,0:T(8,128)(2,1)S(1)} %get-tuple-element.18.q, bf16[4,1536,128]{2,1,0:T(8,128)(2,1)S(1)} %get-tuple-element.19.k, bf16[4,1536,128]{2,1,0:T(8,128)(2,1)S(1)} %get-tuple-element.20.v), custom_call_target="tpu_custom_call" | custom-call | flops 8000000000 | bytes 1048576 | tf_op jit(solution)/shard_map/pallas_call | solution.py:315
  96.2 0.0 collective-permute-done.10.theirs
  96.2 0.0 collective-permute-done.11.their_cols
  96.2 2.8 %shard_map.95 = bf16[512,1024]{1,0:T(8,128)(2,1)} custom-call(s32[4]{0:T(128)S(1)} %compare_select_fusion.1.where, bf16[4,512,128]{2,1,0:T(8,128)(2,1)S(1)} %shard_map.93.mine, bf16[4,512,128]{2,1,0:T(8,128)(2,1)S(1)} %collective-permute-done.10.theirs, bf16[1024,512]{1,0:T(8,128)(2,1)S(1)} %get-tuple-element.21.my_cols, ...), custom_call_target="tpu_custom_call" | custom-call | flops 1000000000 | bytes 1048576 | tf_op jit(solution)/shard_map/pallas_call | solution.py:316
  (2 shorter events, 0.0 us)
Async XLA Ops:
  0.6 28.6 %copy-start = (bf16[1,100,4096]{2,1,0:T(8,128)(2,1)S(1)}, bf16[1,100,4096]{2,1,0:T(8,128)(2,1)}, u32[]{:S(2)}) copy-start(bf16[1,100,4096]{2,1,0:T(8,128)(2,1)} %param.7) | copy-start | bytes 2457604
  1.9 28.7 %collective-permute-start.6 = (bf16[64,2048]{1,0:T(8,128)(2,1)S(1)}, bf16[64,2048]{1,0:T(8,128)(2,1)S(1)}, u32[]{:S(2)}, u32[]{:S(2)}) collective-permute-start(bf16[64,2048]{1,0:T(8,128)(2,1)S(1)} %pad_maximum_fusion.1), channel_id=1, source_target_pairs={{0,64},{1,257},{2,66},{3,259},{4,68},{5,261},{6,70},{7,263},{8,72}... | collective-permute-start | bytes 786440 | tf_op jit(solution)/shard_map/ppermute | solution.py:29
  6.8 23.8 %collective-permute-start.5 = (bf16[64,2048]{1,0:T(8,128)(2,1)S(1)}, bf16[64,2048]{1,0:T(8,128)(2,1)S(1)}, u32[]{:S(2)}, u32[]{:S(2)}) collective-permute-start(bf16[64,2048]{1,0:T(8,128)(2,1)S(1)} %pad_maximum_fusion.1), channel_id=1, source_target_pairs={{0,96},{1,387},{2,98},{3,385},{4,100},{5,391},{6,102},{7,389},{8,1... | collective-permute-start | bytes 786440 | tf_op jit(solution)/shard_map/ppermute | solution.py:29
  8.8 21.9 %collective-permute-start.4 = (bf16[64,2048]{1,0:T(8,128)(2,1)S(1)}, bf16[64,2048]{1,0:T(8,128)(2,1)S(1)}, u32[]{:S(2)}, u32[]{:S(2)}) collective-permute-start(bf16[64,2048]{1,0:T(8,128)(2,1)S(1)} %pad_maximum_fusion.1), channel_id=1, source_target_pairs={{0,32},{1,129},{2,34},{3,131},{4,36},{5,133},{6,38},{7,135},{8,40}... | collective-permute-start | bytes 786440 | tf_op jit(solution)/shard_map/ppermute | solution.py:29
  14.3 25.6 %collective-permute-start = (bf16[100,1024]{1,0:T(8,128)(2,1)}, bf16[100,1024]{1,0:T(8,128)(2,1)}, u32[]{:S(2)}, u32[]{:S(2)}) collective-permute-start(bf16[100,1024]{1,0:T(8,128)(2,1)} %get-tuple-element.23), channel_id=1, source_target_pairs={{0,31},{1,2},{2,1},{3,4},{4,3},{5,6},{6,5},{7,8},{8,7},{9,10},{10,... | collective-permute-start | bytes 614408 | tf_op jit(solution)/shard_map/ppermute | solution.py:52
  20.7 19.1 %collective-permute-start.1 = (bf16[100,1024]{1,0:T(8,128)(2,1)}, bf16[100,1024]{1,0:T(8,128)(2,1)}, u32[]{:S(2)}, u32[]{:S(2)}) collective-permute-start(bf16[100,1024]{1,0:T(8,128)(2,1)} %get-tuple-element.22), channel_id=1, source_target_pairs={{0,1},{1,0},{2,3},{3,2},{4,5},{5,4},{6,7},{7,6},{8,9},{9,8},{10,11... | collective-permute-start | bytes 614408 | tf_op jit(solution)/shard_map/ppermute | solution.py:29
  29.2 10.6 %copy-start.2 = (bf16[32,16,128]{2,1,0:T(8,128)(2,1)S(1)}, bf16[32,16,128]{2,1,0:T(8,128)(2,1)}, u32[]{:S(2)}) copy-start(bf16[32,16,128]{2,1,0:T(8,128)(2,1)} %weight.3) | copy-start | bytes 393220
  29.2 10.6 %copy-start.3 = (s32[32,128]{1,0:T(8,128)S(1)}, s32[32,128]{1,0:T(8,128)}, u32[]{:S(2)}) copy-start(s32[32,128]{1,0:T(8,128)} %index.3) | copy-start | bytes 49156
  30.7 43.2 %collective-permute-start.7 = (bf16[256,2048]{1,0:T(8,128)(2,1)S(1)}, bf16[256,2048]{1,0:T(8,128)(2,1)}, u32[]{:S(2)}, u32[]{:S(2)}) collective-permute-start(bf16[256,2048]{1,0:T(8,128)(2,1)S(1)} %pad_maximum_fusion.own), channel_id=1, source_target_pairs={{0,256},{1,65},{2,258},{3,67},{4,260},{5,69},{6,262},{7,71},{8,264... | collective-permute-start | bytes 3145736 | tf_op jit(solution)/shard_map/ppermute | solution.py:29
  34.5 38.6 %collective-permute-start.8 = (bf16[256,2048]{1,0:T(8,128)(2,1)S(1)}, bf16[256,2048]{1,0:T(8,128)(2,1)S(1)}, u32[]{:S(2)}, u32[]{:S(2)}) collective-permute-start(bf16[256,2048]{1,0:T(8,128)(2,1)S(1)} %pad_maximum_fusion.own), channel_id=1, source_target_pairs={{0,128},{1,33},{2,130},{3,35},{4,132},{5,37},{6,134},{7,39},{8,136... | collective-permute-start | bytes 3145736 | tf_op jit(solution)/shard_map/ppermute | solution.py:29
  36.4 36.7 %collective-permute-start.9 = (bf16[256,2048]{1,0:T(8,128)(2,1)S(1)}, bf16[256,2048]{1,0:T(8,128)(2,1)S(1)}, u32[]{:S(2)}, u32[]{:S(2)}) collective-permute-start(bf16[256,2048]{1,0:T(8,128)(2,1)S(1)} %pad_maximum_fusion.own), channel_id=1, source_target_pairs={{0,386},{1,97},{2,384},{3,99},{4,390},{5,101},{6,388},{7,103},{8,3... | collective-permute-start | bytes 3145736 | tf_op jit(solution)/shard_map/ppermute | solution.py:29
  44.1 21.2 %collective-permute-start.2 = (bf16[256,128]{1,0:T(8,128)(2,1)S(1)}, bf16[256,128]{1,0:T(8,128)(2,1)S(1)}, u32[]{:S(2)}, u32[]{:S(2)}) collective-permute-start(bf16[256,128]{1,0:T(8,128)(2,1)S(1)} %get-tuple-element.12.edge), channel_id=1, source_target_pairs={{0,31},{1,2},{2,1},{3,4},{4,3},{5,6},{6,5},{7,8},{8,7},{9,10},{10,... | collective-permute-start | bytes 196616 | tf_op jit(solution)/shard_map/ppermute | solution.py:52
  50.8 17.1 %copy-start.4 = (f32[1024]{0:T(1024)S(1)}, f32[1024]{0:T(1024)}, u32[]{:S(2)}) copy-start(f32[1024]{0:T(1024)} %param.11) | copy-start | bytes 12292
  66.0 5.1 %collective-permute-start.3 = (bf16[768,128]{1,0:T(8,128)(2,1)}, bf16[768,128]{1,0:T(8,128)(2,1)S(1)}, u32[]{:S(2)}, u32[]{:S(2)}) collective-permute-start(bf16[768,128]{1,0:T(8,128)(2,1)} %pad_maximum_fusion.2), channel_id=1, source_target_pairs={{0,1},{1,0},{2,3},{3,2},{4,5},{5,4},{6,7},{7,6},{8,9},{9,8},{10,11... | collective-permute-start | bytes 589832 | tf_op jit(solution)/shard_map/ppermute | solution.py:29
  67.9 0.9 copy-start.1
  81.7 14.5 %collective-permute-start.11 = (bf16[1024,512]{1,0:T(8,128)(2,1)S(1)}, bf16[1024,512]{1,0:T(8,128)(2,1)S(1)}, u32[]{:S(2)}, u32[]{:S(2)}) collective-permute-start(bf16[1024,512]{1,0:T(8,128)(2,1)S(1)} %get-tuple-element.21.my_cols), channel_id=1, source_target_pairs={{0,1},{1,0},{2,3},{3,2},{4,5},{5,4},{6,7},{7,6},{8,9},{9,8},{10,11... | collective-permute-start | bytes 3145736 | tf_op jit(solution)/shard_map/ppermute | solution.py:29
  89.2 7.0 %collective-permute-start.10 = (bf16[4,512,128]{2,1,0:T(8,128)(2,1)S(1)}, bf16[4,512,128]{2,1,0:T(8,128)(2,1)S(1)}, u32[]{:S(2)}, u32[]{:S(2)}) collective-permute-start(bf16[4,512,128]{2,1,0:T(8,128)(2,1)S(1)} %shard_map.94), channel_id=1, source_target_pairs={{0,1},{1,0},{2,3},{3,2},{4,5},{5,4},{6,7},{7,6},{8,9},{9,8},{10,11... | collective-permute-start | bytes 1572872 | tf_op jit(solution)/shard_map/ppermute | solution.py:29

commit v2 on v1

v2 whole, which is shorter than its diff:
```python
import functools
import math

import jax
import jax.numpy as jnp
from jax import lax
from jax.experimental import pallas as pl
from jax.experimental.pallas import tpu as pltpu
from jax.sharding import PartitionSpec as P


BF, F32 = jnp.bfloat16, jnp.float32
AXES = ("dp", "space")


def coords(dp, s):
    return dp % 4, (s // 2 % 2) * 4 + dp // 4, s // 4, s % 2


def index(x, y, z, c):
    x, y, z = x % 4, y % 8, z % 8
    return ((y % 4) * 4 + x) * 32 + z * 4 + (y // 4) * 2 + c


def send(array, move):
    pairs = [
        (dp * 32 + s, index(*move(*coords(dp, s)))) for dp in range(16) for s in range(32)
    ]
    return lax.ppermute(array, AXES, pairs)


def along(first, shift):
    def move(x, y, z, c):
        return (shift(x), y, z, c) if (c == 0) == first else (x, shift(y), z, c)

    return move


def two(place):
    return place - 2 if place % 2 else place + 2


STEPS = (lambda i: i + 1, lambda i: i - 1, two)
SOURCES = (0, 3, 1, 2)


def swap(array):
    return send(array, lambda x, y, z, c: (x, y, z, 1 - c))


def ring(array, move):
    return lax.ppermute(array, "space", [(s, move(s) % 32) for s in range(32)])


def neighbour(array):
    return ring(array, lambda s: s + 1 if s % 2 else s - 1)


def call(kernel, outs, scratch, flops, limit, n_in, n_smem=0, any_out=()):
    spaces = [pl.ANY if i in any_out else pltpu.VMEM for i in range(len(outs))]
    return pl.pallas_call(
        kernel,
        out_shape=[jax.ShapeDtypeStruct(s, d) for s, d in outs],
        in_specs=[pl.BlockSpec(memory_space=pltpu.SMEM)] * n_smem
        + [pl.BlockSpec(memory_space=pltpu.VMEM)] * n_in,
        out_specs=[pl.BlockSpec(memory_space=m) for m in spaces],
        scratch_shapes=[pltpu.VMEM(*s) if isinstance(s, tuple) else s for s in scratch],
        compiler_params=pltpu.CompilerParams(vmem_limit_bytes=limit << 20),
        cost_estimate=pl.CostEstimate(flops=flops, bytes_accessed=1 << 20, transcendentals=0),
    )


def core_index():
    return lax.rem(lax.axis_index("space"), 2)


def rows_at(start, count=256):
    return pl.ds(pl.multiple_of(start, 256), count)


def dot(a, b):
    return jnp.dot(a, b, preferred_element_type=F32)


def turn(cells, start, table, tall):
    count = cells.shape[1]
    tall[:100, :count] = cells[...].astype(F32)
    for j in range(0, count, 128):
        table[pl.ds(pl.multiple_of(start + j, 128), 128), :] = tall[:, j : j + 128].T


def ends_kernel(cells, near, mate):
    core = core_index()
    near[...] = cells[:, pl.ds(pl.multiple_of(core * 3072, 1024), 1024)]
    mate[...] = cells[:, pl.ds(pl.multiple_of(3072 - core * 3072, 1024), 1024)]


def table_kernel(cells, w_in, table, wide, tall):
    wide[96:, :] = jnp.zeros((32, 1024), BF)
    wide[:100, :] = w_in[...]
    tall[96:, :] = jnp.zeros((32, 1024), F32)

    def part(i, carry):
        at = pl.multiple_of(i * 1024, 1024)
        turn(cells.at[:, pl.ds(at, 1024)], at, table, tall)
        return carry

    lax.fori_loop(0, 4, part, 0)


def encode_blocks(start, index, weight, table, out, at, picked):
    def pair(i, carry):
        for half in range(2):
            local = i * 2 + half
            for j in range(128):
                picked[local, j : j + 1, :] = table[pl.ds(index[start + local, j], 1), :]
        return carry

    lax.fori_loop(0, 8, pair, 0)
    live = lax.broadcasted_iota(jnp.int32, (16, 128), 1) < 100
    for local in range(16):
        summed = dot(weight[start + local], picked[local].astype(BF))
        rows = slice(at + local * 16, at + local * 16 + 16)
        out[rows, :] = jnp.where(live, summed, 0.0).astype(BF)


def encode_edge_kernel(index, weight, near, mate, own, out, table, tall, picked):
    core = core_index()
    table[1024:5120, :] = own[...]
    tall[96:, :] = jnp.zeros((32, 1024), F32)
    turn(near, core * 5120, table, tall)
    turn(mate, 5120 - core * 5120, table, tall)
    encode_blocks(core * 16, index, weight, table, out, 0, picked)


def encode_inner_kernel(index, weight, table, edge, near, out, picked):
    out[:256, :] = edge[...]
    out[512:, :] = near[...]
    encode_blocks(16 - core_index() * 16, index, weight, table, out, 256, picked)


def normalised(encoded, w_in, gain):
    embedded = dot(encoded, w_in)
    average = jnp.mean(embedded, axis=1, keepdims=True)
    centered = embedded - average
    spread = jnp.mean(centered * centered, axis=1, keepdims=True)
    return embedded, (centered * lax.rsqrt(spread + 1e-05) * gain).astype(BF)


def embed_own_kernel(packed, wide, gain, normed, latent):
    at = core_index() * 256
    for row, start in ((0, at), (256, 256 - at)):
        embedded, unit = normalised(packed[row : row + 256, :], wide[...], gain[...])
        normed[rows_at(start), :] = unit
        latent[rows_at(start), :] = embedded.astype(BF)


def embed_rest_kernel(packed, mate, wide, gain, normed):
    at = core_index() * 256
    pieces = ((mate, 0, 256 - at), (mate, 256, at), (mate, 512, 512), (packed, 512, 768))
    for piece, row, start in pieces:
        _, unit = normalised(piece[row : row + 256, :], wide[...], gain[...])
        normed[rows_at(start), :] = unit


def head_ones():
    same = lax.broadcasted_iota(jnp.int32, (256, 256), 0) // 64 == (
        lax.broadcasted_iota(jnp.int32, (256, 256), 1) // 64
    )
    return jnp.where(same, 1.0, 0.0).astype(BF)


def unit_heads(rows, ones):
    parts = []
    for h in range(2):
        part = rows[:, h * 256 : (h + 1) * 256]
        squares = dot((part * part).astype(BF), ones)
        parts.append((part * lax.rsqrt(squares * (1.0 / 64) + 1e-06)).astype(BF))
    return jnp.concatenate(parts, axis=1)


def put_heads(ref, at, rows):
    for p in range(4):
        ref[p, at, :] = rows[:, p * 128 : (p + 1) * 128]


def project_kernel(
    latent, own, rest, here, before, after, across, q, k, v, out_cols, latent_out, weights, sem
):
    copy = pltpu.make_async_copy(latent, latent_out, sem)
    copy.start()
    core = core_index()
    dp = lax.axis_index("dp")
    x, y = lax.rem(dp, 4), lax.div(dp, 4)
    first, second = jnp.where(core == 0, x, y), jnp.where(core == 0, y, x)
    for step, piece in zip(SOURCES, (here, before, after, across)):
        other = lax.rem(second + step, 4)
        for m in range(4):
            mine = lax.rem(first + SOURCES[m], 4)
            block = jnp.where(core == 0, other * 4 + mine, mine * 4 + other)
            rows = slice(m * 64, m * 64 + 64)
            weights[pl.ds(pl.multiple_of(block * 64, 64), 64), :] = piece[rows, :1536]
            half = lax.div(block, 8)
            at = pl.ds(pl.multiple_of(block * 64 - half * 512, 64), 64)
            for j in range(4):
                out_cols[half * 4 + j, at, :] = piece[rows, 1536 + j * 128 : 1664 + j * 128]
    ones = head_ones()
    for rows, start in ((own, core * 512), (rest, 512 - core * 512)):
        rows = rows[:512, :]
        at = rows_at(start + 256, 512)
        put_heads(k, at, unit_heads(dot(rows, weights[:, 512:1024]), ones))
        put_heads(q, rows_at(start, 512), unit_heads(dot(rows, weights[:, :512]), ones))
        put_heads(v, at, dot(rows, weights[:, 1024:]).astype(BF))
    far, near = rows_at(1280 - core * 1280), rows_at(core * 1280)
    rows = rest[512:, :]
    for ref, part in (
        (k, unit_heads(dot(rows, weights[:, 512:1024]), ones)),
        (v, dot(rows, weights[:, 1024:]).astype(BF)),
    ):
        put_heads(ref, far, part[:256])
        put_heads(ref, near, part[256:])
    copy.wait()


def attend_kernel(other, q, k, v, *refs):
    if other:
        cols, out = refs
        out[4:, :, :] = cols[...]
    else:
        (out,) = refs
    core = core_index()
    shard = 1 - core if other else core
    scale = math.log2(math.e) / 8.0
    low = lax.broadcasted_iota(jnp.int32, (512, 128), 1) < 64
    start = pl.multiple_of(shard * 512, 512)

    def tile(p, carry):
        query = q[p, pl.ds(start, 512), :]
        zero = jnp.zeros_like(query)
        heads = (jnp.where(low, query, zero), jnp.where(low, zero, query))
        both = [None, None]
        for at in range(0, 1024, 256):
            keys = k[p, pl.ds(start + at, 256), :]
            wide = jnp.concatenate(
                [v[p, pl.ds(start + at, 256), :], jnp.ones((256, 128), BF)], axis=1
            )
            for h, head in enumerate(heads):
                scores = lax.dot_general(
                    head, keys, (((1,), (1,)), ((), ())), preferred_element_type=F32
                )
                part = dot(jnp.exp2(scores * scale).astype(BF), wide)
                both[h] = part if at == 0 else both[h] + part
        mixed = [b[:, :128] / b[:, 128:] for b in both]
        out[p, :, :] = jnp.where(low, mixed[0], mixed[1]).astype(BF)
        return carry

    lax.fori_loop(0, 4, tile, 0)


def out_kernel(mine, my_cols, theirs, update, done, sem):
    core = core_index()

    def join(ref, first, rows):
        return jnp.concatenate([ref[first + p, rows, :] for p in range(4)], axis=1)

    near = pl.ds(pl.multiple_of(core * 512, 512), 512)
    far = pl.ds(pl.multiple_of(512 - core * 512, 512), 512)
    every = slice(0, 512)
    copies = []
    for i in range(2):
        rows = slice(i * 256, i * 256 + 256)
        here, there = join(mine, 0, rows), join(theirs, 0, rows)
        for ref, skip, at in ((my_cols, 0, near), (theirs, 4, far)):
            top = join(ref, skip + core * 4, every)
            low = join(ref, skip + 4 - core * 4, every)
            done[rows, at] = (dot(here, top) + dot(there, low)).astype(BF)
        copies.append(pltpu.make_async_copy(done.at[rows], update.at[rows], sem.at[i]))
        copies[i].start()
    for copy in copies:
        copy.wait()


def shards(fields, cell_index, interp_weight, w_in, ln_gain, w_qkv, w_out):
    core = core_index()
    even = core == 0
    grid_field = fields[0]
    end = ((100, 1024), BF)
    near_cells, mate_cells = call(ends_kernel, [end, end], [], 100_000_000, 8, 1)(grid_field)
    near_cells = neighbour(near_cells)
    mate_cells = swap(mate_cells)

    halves = [
        jnp.where(even, w[:, i : i + 512], w[:, i + 512 : i + 1024])
        for w, i in ((w_qkv, 0), (w_qkv, 1024), (w_qkv, 2048), (w_out, 0))
    ]
    block = jnp.concatenate(halves, axis=1)
    line = [block]
    for shift in STEPS:
        line.append(send(block, along(True, shift)))
    group = jnp.concatenate(line, axis=0)
    gathered = [group]
    for shift in STEPS:
        gathered.append(send(group, along(False, shift)))

    grown, tall = ((6144, 128), F32), ((128, 1024), F32)
    table, wide = call(
        table_kernel, [((4096, 128), F32), ((128, 1024), BF)], [tall], 2_000_000_000, 8, 2
    )(grid_field, w_in)
    picked = ((16, 128, 128), F32)
    edge, table = call(
        encode_edge_kernel, [((256, 128), BF), grown], [tall, picked], 3_000_000_000, 8, 4, 1
    )(cell_index, interp_weight, near_cells, mate_cells, table)
    near = neighbour(edge)
    (packed,) = call(
        encode_inner_kernel, [((768, 128), BF)], [picked], 3_000_000_000, 8, 4, 1
    )(cell_index, interp_weight, table, edge, near)
    mate = swap(packed)

    gain = ln_gain[None]
    tile = ((512, 1024), BF)
    own_normed, latent = call(
        embed_own_kernel, [tile, tile], [], 1_500_000_000, 12, 3
    )(packed, wide, gain)
    (rest_normed,) = call(
        embed_rest_kernel, [((1024, 1024), BF)], [], 3_000_000_000, 12, 4
    )(packed, mate, wide, gain)
    q, k, v, my_cols, latent = call(
        project_kernel,
        [((4, n, 128), BF) for n in (1024, 1536, 1536)] + [((8, 512, 128), BF), tile],
        [((1024, 1536), BF), pltpu.SemaphoreType.DMA],
        8_000_000_000,
        16,
        7,
        any_out=(4,),
    )(latent, own_normed, rest_normed, *gathered)

    def attend(other, *args):
        kernel = functools.partial(attend_kernel, other)
        outs = [((12 if other else 4, 512, 128), BF)]
        return call(kernel, outs, [], 8_000_000_000, 16, len(args))(*args)[0]

    theirs = swap(attend(True, q, k, v, my_cols))
    mine = attend(False, q, k, v)
    (update,) = call(
        out_kernel,
        [tile],
        [tile, pltpu.SemaphoreType.DMA((2,))],
        1_000_000_000,
        12,
        3,
        any_out=(0,),
    )(mine, my_cols, theirs)
    return latent[None], update[None]


def solution(mesh):
    placed = (
        P("dp", None, "space"),
        P("space", None),
        P("space", None, None),
        P(),
        P(),
        P("dp", None),
        P("dp", None),
    )
    return jax.shard_map(
        shards,
        mesh=mesh,
        in_specs=placed,
        out_specs=(P("dp", "space", None), P("dp", "space", None)),
        check_vma=False,
    )
```

time: 99.5 us -> 92.9 us (0.934)
  the two profiles are of different devices: /device:TPU:11 before, /device:TPU:9 now
where the time goes in v2:
time: 92.9 us; the launch traced here: 92.4 us
  starting transfers between devices  45.2 us (49%)
  Pallas kernels  26.8 us (29%)
  waiting for transfers between devices  16.2 us (17%)
  other arithmetic  2.05 us (2%)
  local copies, waits for them, and re-layouts  1.17 us (1%)
  between operations  0.93 us (1%)
    ppermute x9, starting transfers between devices, send(): return lax.ppermute(array, AXES, pairs)  32 us
    ppermute x2, waiting for transfers between devices, ring(): return lax.ppermute(array, 'space', [(s, move(s) % 32) for s in range(32)])  15.7 us
    ppermute x2, starting transfers between devices, ring(): return lax.ppermute(array, 'space', [(s, move(s) % 32) for s in range(32)])  13.1 us
    pallas_call x2, Pallas kernels, attend(): return call(kernel, outs, [], 8000000000, 16, len(args))(*args)[0]  10.2 us
    pallas_call x1, Pallas kernels, shards(): call(project_kernel, [((4, n, 128), BF) for n in (1024, 1536, 1536)] + [(...  5.6 us
    pallas_call x1, Pallas kernels, shards(): call(encode_edge_kernel, [((256, 128), BF), grown], [tall, picked], 30000...  3.07 us
    pallas_call x1, Pallas kernels, shards(): call(encode_inner_kernel, [((768, 128), BF)], [picked], 3000000000, 8, 4, 1)  2.72 us
    pallas_call x1, Pallas kernels, shards(): call(out_kernel, [tile], [tile, pltpu.SemaphoreType.DMA((2,))], 100000000...  2.08 us
  transfers between devices with their start and end apart: 11, of which 2 were waited for; matrix products, arithmetic and copies ran while one was open for 0% of the time, Pallas kernels for 15%

profile of v2, /device:TPU:9, one launch (start us, length us, event | category | flops | bytes accessed | tf_op | source)
XLA Modules:
  0.0 92.4 jit_solution(18122506143126906000)
XLA Ops:
  0.6 0.0 copy-start.1
  0.6 0.9 slice_select_fusion
  1.6 1.0 %slice_select_fusion.3 = (bf16[64,512]{1,0:T(8,128)(2,1)S(1)}, bf16[64,512]{1,0:T(8,128)(2,1)S(1)}, bf16[64,512]{1,0:T(8,128)(2,1)S(1)}) fusion(bf16[64,3072]{1,0:T(8,128)(2,1)} %param.12, pred[]{:T(512)S(6)} %eq.3), kind=kLoop, calls=%fused_computation.5 | loop fusion | flops 98304 | bytes 589825 | tf_op jit(solution)/shard_map/jit(_where)/select_n | solution.py:293
  2.6 5.0 %collective-permute-start.6 = (bf16[64,2048]{1,0:T(8,128)(2,1)S(1)}, bf16[64,2048]{1,0:T(8,128)(2,1)S(1)}, u32[]{:S(2)}, u32[]{:S(2)}) collective-permute-start(bf16[64,2048]{1,0:T(8,128)(2,1)S(1)} %pad_maximum_fusion.1), channel_id=1, source_target_pairs={{0,64},{1,257},{2,66},{3,259},{4,68},{5,261},{6,70},{7,263},{8,72}... | collective-permute-start | bytes 786440 | tf_op jit(solution)/shard_map/ppermute | solution.py:29
  7.6 1.9 %collective-permute-start.5 = (bf16[64,2048]{1,0:T(8,128)(2,1)S(1)}, bf16[64,2048]{1,0:T(8,128)(2,1)S(1)}, u32[]{:S(2)}, u32[]{:S(2)}) collective-permute-start(bf16[64,2048]{1,0:T(8,128)(2,1)S(1)} %pad_maximum_fusion.1), channel_id=1, source_target_pairs={{0,96},{1,387},{2,98},{3,385},{4,100},{5,391},{6,102},{7,389},{8,1... | collective-permute-start | bytes 786440 | tf_op jit(solution)/shard_map/ppermute | solution.py:29
  9.6 3.6 %collective-permute-start.4 = (bf16[64,2048]{1,0:T(8,128)(2,1)S(1)}, bf16[64,2048]{1,0:T(8,128)(2,1)S(1)}, u32[]{:S(2)}, u32[]{:S(2)}) collective-permute-start(bf16[64,2048]{1,0:T(8,128)(2,1)S(1)} %pad_maximum_fusion.1), channel_id=1, source_target_pairs={{0,32},{1,129},{2,34},{3,131},{4,36},{5,133},{6,38},{7,135},{8,40}... | collective-permute-start | bytes 786440 | tf_op jit(solution)/shard_map/ppermute | solution.py:29
  13.2 0.0 copy-start
  13.2 1.1 %copy-done = bf16[1,100,4096]{2,1,0:T(8,128)(2,1)S(1)} copy-done((bf16[1,100,4096]{2,1,0:T(8,128)(2,1)S(1)}, bf16[1,100,4096]{2,1,0:T(8,128)(2,1)}, u32[]{:S(2)}) %copy-start) | copy-done | bytes 819224
  14.4 7.3 %collective-permute-start = (bf16[100,1024]{1,0:T(8,128)(2,1)S(1)}, bf16[100,1024]{1,0:T(8,128)(2,1)S(1)}, u32[]{:S(2)}, u32[]{:S(2)}) collective-permute-start(bf16[100,1024]{1,0:T(8,128)(2,1)S(1)} %get-tuple-element.15), channel_id=1, source_target_pairs={{0,31},{1,2},{2,1},{3,4},{4,3},{5,6},{6,5},{7,8},{8,7},{9,10},{10,... | collective-permute-start | bytes 614408 | tf_op jit(solution)/shard_map/ppermute | solution.py:52
  21.7 7.6 %collective-permute-start.1 = (bf16[100,1024]{1,0:T(8,128)(2,1)S(1)}, bf16[100,1024]{1,0:T(8,128)(2,1)S(1)}, u32[]{:S(2)}, u32[]{:S(2)}) collective-permute-start(bf16[100,1024]{1,0:T(8,128)(2,1)S(1)} %get-tuple-element.16), channel_id=1, source_target_pairs={{0,1},{1,0},{2,3},{3,2},{4,5},{5,4},{6,7},{7,6},{8,9},{9,8},{10,11... | collective-permute-start | bytes 614408 | tf_op jit(solution)/shard_map/ppermute | solution.py:29
  29.3 0.0 copy-done.1
  29.4 0.8 shard_map.87
  30.2 0.0 copy-start.2
  30.2 0.0 copy-start.3
  30.2 0.0 collective-permute-done.6
  30.2 0.0 collective-permute-done.5
  30.2 0.0 collective-permute-done.4
  30.2 0.1 pad_maximum_fusion.here
  30.3 4.7 %collective-permute-start.9 = (bf16[256,2048]{1,0:T(8,128)(2,1)S(1)}, bf16[256,2048]{1,0:T(8,128)(2,1)S(1)}, u32[]{:S(2)}, u32[]{:S(2)}) collective-permute-start(bf16[256,2048]{1,0:T(8,128)(2,1)S(1)} %pad_maximum_fusion.here), channel_id=1, source_target_pairs={{0,256},{1,65},{2,258},{3,67},{4,260},{5,69},{6,262},{7,71},{8,264... | collective-permute-start | bytes 3145736 | tf_op jit(solution)/shard_map/ppermute | solution.py:29
  35.0 2.8 %collective-permute-start.8 = (bf16[256,2048]{1,0:T(8,128)(2,1)S(1)}, bf16[256,2048]{1,0:T(8,128)(2,1)S(1)}, u32[]{:S(2)}, u32[]{:S(2)}) collective-permute-start(bf16[256,2048]{1,0:T(8,128)(2,1)S(1)} %pad_maximum_fusion.here), channel_id=1, source_target_pairs={{0,386},{1,97},{2,384},{3,99},{4,390},{5,101},{6,388},{7,103},{8,3... | collective-permute-start | bytes 3145736 | tf_op jit(solution)/shard_map/ppermute | solution.py:29
  37.8 2.5 %collective-permute-start.7 = (bf16[256,2048]{1,0:T(8,128)(2,1)S(1)}, bf16[256,2048]{1,0:T(8,128)(2,1)S(1)}, u32[]{:S(2)}, u32[]{:S(2)}) collective-permute-start(bf16[256,2048]{1,0:T(8,128)(2,1)S(1)} %pad_maximum_fusion.here), channel_id=1, source_target_pairs={{0,128},{1,33},{2,130},{3,35},{4,132},{5,37},{6,134},{7,39},{8,136... | collective-permute-start | bytes 3145736 | tf_op jit(solution)/shard_map/ppermute | solution.py:29
  40.3 0.0 collective-permute-done.near
  40.3 0.0 collective-permute-done.1.mate
  40.3 0.0 copy-done.2
  40.3 0.0 copy-done.3
  40.3 3.1 %shard_map.88 = (bf16[256,128]{1,0:T(8,128)(2,1)S(1)}, f32[6144,128]{1,0:T(8,128)S(1)}) custom-call(s32[32,128]{1,0:T(8,128)S(1)} %copy-done.3, bf16[32,16,128]{2,1,0:T(8,128)(2,1)S(1)} %copy-done.2, bf16[100,1024]{1,0:T(8,128)(2,1)S(1)} %collective-permute-done.near, bf16[100,1024]{1,0:T(8,128)(2,1)S(1)} %collective-permute-done.1.mate, ...), custom_call_target="tpu_custom_call" | custom-call | flops 3000000000 | bytes 1048576 | tf_op jit(solution)/shard_map/pallas_call | solution.py:310
  43.4 5.8 %collective-permute-start.2 = (bf16[256,128]{1,0:T(8,128)(2,1)S(1)}, bf16[256,128]{1,0:T(8,128)(2,1)S(1)}, u32[]{:S(2)}, u32[]{:S(2)}) collective-permute-start(bf16[256,128]{1,0:T(8,128)(2,1)S(1)} %get-tuple-element.19.edge), channel_id=1, source_target_pairs={{0,31},{1,2},{2,1},{3,4},{4,3},{5,6},{6,5},{7,8},{8,7},{9,10},{10,... | collective-permute-start | bytes 196616 | tf_op jit(solution)/shard_map/ppermute | solution.py:52
  49.2 15.7 %collective-permute-done.2.near = bf16[256,128]{1,0:T(8,128)(2,1)S(1)} collective-permute-done((bf16[256,128]{1,0:T(8,128)(2,1)S(1)}, bf16[256,128]{1,0:T(8,128)(2,1)S(1)}, u32[]{:S(2)}, u32[]{:S(2)}) %collective-permute-start.2) | collective-permute-done | bytes 65568 | tf_op jit(solution)/shard_map/ppermute | solution.py:52
  64.9 0.0 copy-start.4
  64.9 2.7 %shard_map.89.packed = bf16[768,128]{1,0:T(8,128)(2,1)S(1)} custom-call(s32[32,128]{1,0:T(8,128)S(1)} %copy-done.3, bf16[32,16,128]{2,1,0:T(8,128)(2,1)S(1)} %copy-done.2, f32[6144,128]{1,0:T(8,128)S(1)} %get-tuple-element.18.table, bf16[256,128]{1,0:T(8,128)(2,1)S(1)} %get-tuple-element.19.edge, bf16[256,128]{1,0:T(8,128)(2,1)S(1)} %collective-permute-done.2.near), custom_call_target="tpu_custom_call" | custom-call | flops 3000000000 | bytes 1048576 | tf_op jit(solution)/shard_map/pallas_call | solution.py:314
  67.6 1.9 %collective-permute-start.3 = (bf16[768,128]{1,0:T(8,128)(2,1)S(1)}, bf16[768,128]{1,0:T(8,128)(2,1)S(1)}, u32[]{:S(2)}, u32[]{:S(2)}) collective-permute-start(bf16[768,128]{1,0:T(8,128)(2,1)S(1)} %shard_map.89.packed), channel_id=1, source_target_pairs={{0,1},{1,0},{2,3},{3,2},{4,5},{5,4},{6,7},{7,6},{8,9},{9,8},{10,11... | collective-permute-start | bytes 589832 | tf_op jit(solution)/shard_map/ppermute | solution.py:29
  69.5 0.0 copy-done.4
  69.5 0.8 shard_map.90
  70.4 0.6 collective-permute-done.3.mate
  70.9 1.5 %shard_map.91.rest = bf16[1024,1024]{1,0:T(8,128)(2,1)S(1)} custom-call(bf16[768,128]{1,0:T(8,128)(2,1)S(1)} %shard_map.89.packed, bf16[768,128]{1,0:T(8,128)(2,1)S(1)} %collective-permute-done.3.mate, bf16[128,1024]{1,0:T(8,128)(2,1)S(1)} %get-tuple-element.20.wide, f32[1,1024]{1,0:T(1,128)S(1)} %bitcast.7), custom_call_target="tpu_custom_call" | custom-call | flops 3000000000 | bytes 1048576 | tf_op jit(solution)/shard_map/pallas_call | solution.py:324
  72.4 0.0 collective-permute-done.9.across
  72.4 0.0 collective-permute-done.8.after
  72.4 0.0 collective-permute-done.7.before
  72.4 5.6 %shard_map.92 = (bf16[4,1024,128]{2,1,0:T(8,128)(2,1)S(1)}, bf16[4,1536,128]{2,1,0:T(8,128)(2,1)S(1)}, bf16[4,1536,128]{2,1,0:T(8,128)(2,1)S(1)}, bf16[8,512,128]{2,1,0:T(8,128)(2,1)S(1)}, bf16[512,1024]{1,0:T(8,128)(2,1)}) custom-call(bf16[512,1024]{1,0:T(8,128)(2,1)S(1)} %get-tuple-element.21.latent, bf16[512,1024]{1,0:T(8,128)(2,1)S(1)} %get-tuple-element.22.own, ...), custom_call_target="tpu_custom_call" | custom-call | flops 8000000000 | bytes 1048576 | tf_op jit(solution)/shard_map/pallas_call | solution.py:327
  78.0 5.1 %shard_map.94 = bf16[12,512,128]{2,1,0:T(8,128)(2,1)S(1)} custom-call(bf16[4,1024,128]{2,1,0:T(8,128)(2,1)S(1)} %get-tuple-element.24.q, bf16[4,1536,128]{2,1,0:T(8,128)(2,1)S(1)} %get-tuple-element.25.k, bf16[4,1536,128]{2,1,0:T(8,128)(2,1)S(1)} %get-tuple-element.26.v, bf16[8,512,128]{2,1,0:T(8,128)(2,1)S(1)} %get-tuple-element.27.refs_0_.my_cols), custom_call_target="tpu_custom_call" | custom-call | flops 8000000000 | bytes 1048576 | tf_op jit(solution)/shard_map/pallas_call | solution.py:340
  83.2 2.1 %collective-permute-start.10 = (bf16[12,512,128]{2,1,0:T(8,128)(2,1)S(1)}, bf16[12,512,128]{2,1,0:T(8,128)(2,1)S(1)}, u32[]{:S(2)}, u32[]{:S(2)}) collective-permute-start(bf16[12,512,128]{2,1,0:T(8,128)(2,1)S(1)} %shard_map.94), channel_id=1, source_target_pairs={{0,1},{1,0},{2,3},{3,2},{4,5},{5,4},{6,7},{7,6},{8,9},{9,8},{10,11... | collective-permute-start | bytes 4718600 | tf_op jit(solution)/shard_map/ppermute | solution.py:29
  85.2 5.1 %shard_map.93.mine = bf16[4,512,128]{2,1,0:T(8,128)(2,1)S(1)} custom-call(bf16[4,1024,128]{2,1,0:T(8,128)(2,1)S(1)} %get-tuple-element.24.q, bf16[4,1536,128]{2,1,0:T(8,128)(2,1)S(1)} %get-tuple-element.25.k, bf16[4,1536,128]{2,1,0:T(8,128)(2,1)S(1)} %get-tuple-element.26.v), custom_call_target="tpu_custom_call" | custom-call | flops 8000000000 | bytes 1048576 | tf_op jit(solution)/shard_map/pallas_call | solution.py:340
  90.3 0.0 collective-permute-done.10.theirs
  90.3 2.1 %shard_map.95 = bf16[512,1024]{1,0:T(8,128)(2,1)} custom-call(bf16[4,512,128]{2,1,0:T(8,128)(2,1)S(1)} %shard_map.93.mine, bf16[8,512,128]{2,1,0:T(8,128)(2,1)S(1)} %get-tuple-element.27.refs_0_.my_cols, bf16[12,512,128]{2,1,0:T(8,128)(2,1)S(1)} %collective-permute-done.10.theirs), custom_call_target="tpu_custom_call" | custom-call | flops 1000000000 | bytes 1048576 | tf_op jit(solution)/shard_map/pallas_call | solution.py:344
  (2 shorter events, 0.0 us)
Async XLA Ops:
  0.6 28.7 %copy-start.1 = (bf16[100,1024]{1,0:T(8,128)(2,1)S(1)}, bf16[100,1024]{1,0:T(8,128)(2,1)}, u32[]{:S(2)}) copy-start(bf16[100,1024]{1,0:T(8,128)(2,1)} %w_in.1) | copy-start | bytes 614404
  2.6 27.6 %collective-permute-start.6 = (bf16[64,2048]{1,0:T(8,128)(2,1)S(1)}, bf16[64,2048]{1,0:T(8,128)(2,1)S(1)}, u32[]{:S(2)}, u32[]{:S(2)}) collective-permute-start(bf16[64,2048]{1,0:T(8,128)(2,1)S(1)} %pad_maximum_fusion.1), channel_id=1, source_target_pairs={{0,64},{1,257},{2,66},{3,259},{4,68},{5,261},{6,70},{7,263},{8,72}... | collective-permute-start | bytes 786440 | tf_op jit(solution)/shard_map/ppermute | solution.py:29
  7.6 22.6 %collective-permute-start.5 = (bf16[64,2048]{1,0:T(8,128)(2,1)S(1)}, bf16[64,2048]{1,0:T(8,128)(2,1)S(1)}, u32[]{:S(2)}, u32[]{:S(2)}) collective-permute-start(bf16[64,2048]{1,0:T(8,128)(2,1)S(1)} %pad_maximum_fusion.1), channel_id=1, source_target_pairs={{0,96},{1,387},{2,98},{3,385},{4,100},{5,391},{6,102},{7,389},{8,1... | collective-permute-start | bytes 786440 | tf_op jit(solution)/shard_map/ppermute | solution.py:29
  9.6 20.7 %collective-permute-start.4 = (bf16[64,2048]{1,0:T(8,128)(2,1)S(1)}, bf16[64,2048]{1,0:T(8,128)(2,1)S(1)}, u32[]{:S(2)}, u32[]{:S(2)}) collective-permute-start(bf16[64,2048]{1,0:T(8,128)(2,1)S(1)} %pad_maximum_fusion.1), channel_id=1, source_target_pairs={{0,32},{1,129},{2,34},{3,131},{4,36},{5,133},{6,38},{7,135},{8,40}... | collective-permute-start | bytes 786440 | tf_op jit(solution)/shard_map/ppermute | solution.py:29
  13.2 1.2 %copy-start = (bf16[1,100,4096]{2,1,0:T(8,128)(2,1)S(1)}, bf16[1,100,4096]{2,1,0:T(8,128)(2,1)}, u32[]{:S(2)}) copy-start(bf16[1,100,4096]{2,1,0:T(8,128)(2,1)} %param.7) | copy-start | bytes 2457604
  14.4 25.9 %collective-permute-start = (bf16[100,1024]{1,0:T(8,128)(2,1)S(1)}, bf16[100,1024]{1,0:T(8,128)(2,1)S(1)}, u32[]{:S(2)}, u32[]{:S(2)}) collective-permute-start(bf16[100,1024]{1,0:T(8,128)(2,1)S(1)} %get-tuple-element.15), channel_id=1, source_target_pairs={{0,31},{1,2},{2,1},{3,4},{4,3},{5,6},{6,5},{7,8},{8,7},{9,10},{10,... | collective-permute-start | bytes 614408 | tf_op jit(solution)/shard_map/ppermute | solution.py:52
  21.7 18.6 %collective-permute-start.1 = (bf16[100,1024]{1,0:T(8,128)(2,1)S(1)}, bf16[100,1024]{1,0:T(8,128)(2,1)S(1)}, u32[]{:S(2)}, u32[]{:S(2)}) collective-permute-start(bf16[100,1024]{1,0:T(8,128)(2,1)S(1)} %get-tuple-element.16), channel_id=1, source_target_pairs={{0,1},{1,0},{2,3},{3,2},{4,5},{5,4},{6,7},{7,6},{8,9},{9,8},{10,11... | collective-permute-start | bytes 614408 | tf_op jit(solution)/shard_map/ppermute | solution.py:29
  30.2 10.1 %copy-start.2 = (bf16[32,16,128]{2,1,0:T(8,128)(2,1)S(1)}, bf16[32,16,128]{2,1,0:T(8,128)(2,1)}, u32[]{:S(2)}) copy-start(bf16[32,16,128]{2,1,0:T(8,128)(2,1)} %weight.3) | copy-start | bytes 393220
  30.2 10.1 %copy-start.3 = (s32[32,128]{1,0:T(8,128)S(1)}, s32[32,128]{1,0:T(8,128)}, u32[]{:S(2)}) copy-start(s32[32,128]{1,0:T(8,128)} %index.3) | copy-start | bytes 49156
  30.3 42.1 %collective-permute-start.9 = (bf16[256,2048]{1,0:T(8,128)(2,1)S(1)}, bf16[256,2048]{1,0:T(8,128)(2,1)S(1)}, u32[]{:S(2)}, u32[]{:S(2)}) collective-permute-start(bf16[256,2048]{1,0:T(8,128)(2,1)S(1)} %pad_maximum_fusion.here), channel_id=1, source_target_pairs={{0,256},{1,65},{2,258},{3,67},{4,260},{5,69},{6,262},{7,71},{8,264... | collective-permute-start | bytes 3145736 | tf_op jit(solution)/shard_map/ppermute | solution.py:29
  35.0 37.4 %collective-permute-start.8 = (bf16[256,2048]{1,0:T(8,128)(2,1)S(1)}, bf16[256,2048]{1,0:T(8,128)(2,1)S(1)}, u32[]{:S(2)}, u32[]{:S(2)}) collective-permute-start(bf16[256,2048]{1,0:T(8,128)(2,1)S(1)} %pad_maximum_fusion.here), channel_id=1, source_target_pairs={{0,386},{1,97},{2,384},{3,99},{4,390},{5,101},{6,388},{7,103},{8,3... | collective-permute-start | bytes 3145736 | tf_op jit(solution)/shard_map/ppermute | solution.py:29
  37.8 34.7 %collective-permute-start.7 = (bf16[256,2048]{1,0:T(8,128)(2,1)S(1)}, bf16[256,2048]{1,0:T(8,128)(2,1)S(1)}, u32[]{:S(2)}, u32[]{:S(2)}) collective-permute-start(bf16[256,2048]{1,0:T(8,128)(2,1)S(1)} %pad_maximum_fusion.here), channel_id=1, source_target_pairs={{0,128},{1,33},{2,130},{3,35},{4,132},{5,37},{6,134},{7,39},{8,136... | collective-permute-start | bytes 3145736 | tf_op jit(solution)/shard_map/ppermute | solution.py:29
  43.4 21.5 %collective-permute-start.2 = (bf16[256,128]{1,0:T(8,128)(2,1)S(1)}, bf16[256,128]{1,0:T(8,128)(2,1)S(1)}, u32[]{:S(2)}, u32[]{:S(2)}) collective-permute-start(bf16[256,128]{1,0:T(8,128)(2,1)S(1)} %get-tuple-element.19.edge), channel_id=1, source_target_pairs={{0,31},{1,2},{2,1},{3,4},{4,3},{5,6},{6,5},{7,8},{8,7},{9,10},{10,... | collective-permute-start | bytes 196616 | tf_op jit(solution)/shard_map/ppermute | solution.py:52
  64.9 4.7 %copy-start.4 = (f32[1024]{0:T(1024)S(1)}, f32[1024]{0:T(1024)}, u32[]{:S(2)}) copy-start(f32[1024]{0:T(1024)} %param.11) | copy-start | bytes 12292
  67.6 3.3 %collective-permute-start.3 = (bf16[768,128]{1,0:T(8,128)(2,1)S(1)}, bf16[768,128]{1,0:T(8,128)(2,1)S(1)}, u32[]{:S(2)}, u32[]{:S(2)}) collective-permute-start(bf16[768,128]{1,0:T(8,128)(2,1)S(1)} %shard_map.89.packed), channel_id=1, source_target_pairs={{0,1},{1,0},{2,3},{3,2},{4,5},{5,4},{6,7},{7,6},{8,9},{9,8},{10,11... | collective-permute-start | bytes 589832 | tf_op jit(solution)/shard_map/ppermute | solution.py:29
  83.2 7.1 %collective-permute-start.10 = (bf16[12,512,128]{2,1,0:T(8,128)(2,1)S(1)}, bf16[12,512,128]{2,1,0:T(8,128)(2,1)S(1)}, u32[]{:S(2)}, u32[]{:S(2)}) collective-permute-start(bf16[12,512,128]{2,1,0:T(8,128)(2,1)S(1)} %shard_map.94), channel_id=1, source_target_pairs={{0,1},{1,0},{2,3},{3,2},{4,5},{5,4},{6,7},{7,6},{8,9},{9,8},{10,11... | collective-permute-start | bytes 4718600 | tf_op jit(solution)/shard_map/ppermute | solution.py:29

commit v3 on v2

--- a/solution.py
+++ b/solution.py
@@ -56,12 +56,13 @@
     return ring(array, lambda s: s + 1 if s % 2 else s - 1)
 
 
-def call(kernel, outs, scratch, flops, limit, n_in, n_smem=0, any_out=()):
+def call(kernel, outs, scratch, flops, limit, n_in, n_smem=0, any_out=(), n_hbm=0):
     spaces = [pl.ANY if i in any_out else pltpu.VMEM for i in range(len(outs))]
     return pl.pallas_call(
         kernel,
         out_shape=[jax.ShapeDtypeStruct(s, d) for s, d in outs],
         in_specs=[pl.BlockSpec(memory_space=pltpu.SMEM)] * n_smem
+        + [pl.BlockSpec(memory_space=pltpu.HBM)] * n_hbm
         + [pl.BlockSpec(memory_space=pltpu.VMEM)] * n_in,
         out_specs=[pl.BlockSpec(memory_space=m) for m in spaces],
         scratch_shapes=[pltpu.VMEM(*s) if isinstance(s, tuple) else s for s in scratch],
@@ -89,10 +90,27 @@
         table[pl.ds(pl.multiple_of(start + j, 128), 128), :] = tall[:, j : j + 128].T
 
 
-def ends_kernel(cells, near, mate):
-    core = core_index()
-    near[...] = cells[:, pl.ds(pl.multiple_of(core * 3072, 1024), 1024)]
-    mate[...] = cells[:, pl.ds(pl.multiple_of(3072 - core * 3072, 1024), 1024)]
+def front_kernel(fields, w_qkv, w_out, block, near, mate, cells, sem):
+    core = core_index()
+
+    def part(source, start, count):
+        return source.at[:, pl.ds(pl.multiple_of(start, 128), count)]
+
+    moves = [
+        (part(w_qkv, i * 1024 + core * 512, 512), block.at[:, i * 512 : i * 512 + 512])
+        for i in range(3)
+    ]
+    moves += [
+        (part(w_out, core * 512, 512), block.at[:, 1536:]),
+        (part(fields, core * 3072, 1024), near),
+        (part(fields, 3072 - core * 3072, 1024), mate),
+        (fields, cells),
+    ]
+    copies = [pltpu.make_async_copy(a, b, sem.at[i]) for i, (a, b) in enumerate(moves)]
+    for copy in copies:
+        copy.start()
+    for copy in copies:
+        copy.wait()
 
 
 def table_kernel(cells, w_in, table, wide, tall):
@@ -108,7 +126,7 @@
     lax.fori_loop(0, 4, part, 0)
 
 
-def encode_blocks(start, index, weight, table, out, at, picked):
+def encode_blocks(start, index, weight, table, out, picked):
     def pair(i, carry):
         for half in range(2):
             local = i * 2 + half
@@ -120,7 +138,7 @@
     live = lax.broadcasted_iota(jnp.int32, (16, 128), 1) < 100
     for local in range(16):
         summed = dot(weight[start + local], picked[local].astype(BF))
-        rows = slice(at + local * 16, at + local * 16 + 16)
+        rows = slice(local * 16, local * 16 + 16)
         out[rows, :] = jnp.where(live, summed, 0.0).astype(BF)
 
 
@@ -130,13 +148,11 @@
     tall[96:, :] = jnp.zeros((32, 1024), F32)
     turn(near, core * 5120, table, tall)
     turn(mate, 5120 - core * 5120, table, tall)
-    encode_blocks(core * 16, index, weight, table, out, 0, picked)
-
-
-def encode_inner_kernel(index, weight, table, edge, near, out, picked):
-    out[:256, :] = edge[...]
-    out[512:, :] = near[...]
-    encode_blocks(16 - core_index() * 16, index, weight, table, out, 256, picked)
+    encode_blocks(core * 16, index, weight, table, out, picked)
+
+
+def encode_inner_kernel(index, weight, table, out, picked):
+    encode_blocks(16 - core_index() * 16, index, weight, table, out, picked)
 
 
 def normalised(encoded, w_in, gain):
@@ -281,19 +297,19 @@
 
 
 def shards(fields, cell_index, interp_weight, w_in, ln_gain, w_qkv, w_out):
-    core = core_index()
-    even = core == 0
-    grid_field = fields[0]
     end = ((100, 1024), BF)
-    near_cells, mate_cells = call(ends_kernel, [end, end], [], 100_000_000, 8, 1)(grid_field)
+    block, near_cells, mate_cells, cells = call(
+        front_kernel,
+        [((64, 2048), BF), end, end, ((100, 4096), BF)],
+        [pltpu.SemaphoreType.DMA((7,))],
+        100_000_000,
+        8,
+        0,
+        n_hbm=3,
+    )(*(pltpu.with_memory_space_constraint(a, pltpu.HBM) for a in (fields[0], w_qkv, w_out)))
     near_cells = neighbour(near_cells)
     mate_cells = swap(mate_cells)
 
-    halves = [
-        jnp.where(even, w[:, i : i + 512], w[:, i + 512 : i + 1024])
-        for w, i in ((w_qkv, 0), (w_qkv, 1024), (w_qkv, 2048), (w_out, 0))
-    ]
-    block = jnp.concatenate(halves, axis=1)
     line = [block]
     for shift in STEPS:
         line.append(send(block, along(True, shift)))
@@ -305,15 +321,16 @@
     grown, tall = ((6144, 128), F32), ((128, 1024), F32)
     table, wide = call(
         table_kernel, [((4096, 128), F32), ((128, 1024), BF)], [tall], 2_000_000_000, 8, 2
-    )(grid_field, w_in)
+    )(cells, w_in)
     picked = ((16, 128, 128), F32)
     edge, table = call(
         encode_edge_kernel, [((256, 128), BF), grown], [tall, picked], 3_000_000_000, 8, 4, 1
     )(cell_index, interp_weight, near_cells, mate_cells, table)
     near = neighbour(edge)
-    (packed,) = call(
-        encode_inner_kernel, [((768, 128), BF)], [picked], 3_000_000_000, 8, 4, 1
-    )(cell_index, interp_weight, table, edge, near)
+    (inner,) = call(
+        encode_inner_kernel, [((256, 128), BF)], [picked], 3_000_000_000, 8, 2, 1
+    )(cell_index, interp_weight, table)
+    packed = jnp.concatenate([edge, inner, near], axis=0)
     mate = swap(packed)
 
     gain = ln_gain[None]

time: 92.9 us -> 88.6 us (0.954)
  the two profiles are of different devices: /device:TPU:9 before, /device:TPU:11 now
where the time goes in v3:
time: 88.6 us; the launch traced here: 88.1 us
  starting transfers between devices  45.2 us (51%)
  Pallas kernels  28.4 us (32%)
  waiting for transfers between devices  13.5 us (15%)
  between operations  0.94 us (1%)
    ppermute x9, starting transfers between devices, send(): return lax.ppermute(array, AXES, pairs)  32 us
    ppermute x2, starting transfers between devices, ring(): return lax.ppermute(array, 'space', [(s, move(s) % 32) for s in range(32)])  13.1 us
    ppermute x2, waiting for transfers between devices, ring(): return lax.ppermute(array, 'space', [(s, move(s) % 32) for s in range(32)])  12.9 us
    pallas_call x2, Pallas kernels, attend(): return call(kernel, outs, [], 8000000000, 16, len(args))(*args)[0]  10.2 us
    pallas_call x1, Pallas kernels, shards(): call(project_kernel, [((4, n, 128), BF) for n in (1024, 1536, 1536)] + [(...  5.6 us
    pallas_call x1, Pallas kernels, shards(): call(encode_edge_kernel, [((256, 128), BF), grown], [tall, picked], 30000...  3.07 us
    pallas_call x1, Pallas kernels, shards(): call(encode_inner_kernel, [((256, 128), BF)], [picked], 3000000000, 8, 2, 1)  2.72 us
    pallas_call x1, Pallas kernels, shards(): call(out_kernel, [tile], [tile, pltpu.SemaphoreType.DMA((2,))], 100000000...  2.08 us
  transfers between devices with their start and end apart: 11, of which 2 were waited for; matrix products, arithmetic and copies ran while one was open for 0% of the time, Pallas kernels for 16%

profile of v3, /device:TPU:11, one launch (start us, length us, event | category | flops | bytes accessed | tf_op | source)
XLA Modules:
  0.0 88.1 jit_solution(15561638226405199931)
XLA Ops:
  0.6 0.0 copy-start
  0.6 1.6 %shard_map.86 = (bf16[64,2048]{1,0:T(8,128)(2,1)S(1)}, bf16[100,1024]{1,0:T(8,128)(2,1)S(1)}, bf16[100,1024]{1,0:T(8,128)(2,1)S(1)}, bf16[100,4096]{1,0:T(8,128)(2,1)S(1)}) custom-call(bf16[100,4096]{1,0:T(8,128)(2,1)} %bitcast.7, bf16[64,3072]{1,0:T(8,128)(2,1)} %w_qkv.1, bf16[64,1024]{1,0:T(8,128)(2,1)} %w_out.1), custom_call_target="tpu_custom_call" | custom-call | flops 100000000 | bytes 1048576 | tf_op jit(solution)/shard_map/pallas_call | solution.py:301
  2.3 5.0 %collective-permute-start.6 = (bf16[64,2048]{1,0:T(8,128)(2,1)S(1)}, bf16[64,2048]{1,0:T(8,128)(2,1)S(1)}, u32[]{:S(2)}, u32[]{:S(2)}) collective-permute-start(bf16[64,2048]{1,0:T(8,128)(2,1)S(1)} %get-tuple-element.26), channel_id=1, source_target_pairs={{0,64},{1,257},{2,66},{3,259},{4,68},{5,261},{6,70},{7,263},{8,72}... | collective-permute-start | bytes 786440 | tf_op jit(solution)/shard_map/ppermute | solution.py:29
  7.3 1.9 %collective-permute-start.5 = (bf16[64,2048]{1,0:T(8,128)(2,1)S(1)}, bf16[64,2048]{1,0:T(8,128)(2,1)S(1)}, u32[]{:S(2)}, u32[]{:S(2)}) collective-permute-start(bf16[64,2048]{1,0:T(8,128)(2,1)S(1)} %get-tuple-element.26), channel_id=1, source_target_pairs={{0,96},{1,387},{2,98},{3,385},{4,100},{5,391},{6,102},{7,389},{8,1... | collective-permute-start | bytes 786440 | tf_op jit(solution)/shard_map/ppermute | solution.py:29
  9.2 3.6 %collective-permute-start.4 = (bf16[64,2048]{1,0:T(8,128)(2,1)S(1)}, bf16[64,2048]{1,0:T(8,128)(2,1)S(1)}, u32[]{:S(2)}, u32[]{:S(2)}) collective-permute-start(bf16[64,2048]{1,0:T(8,128)(2,1)S(1)} %get-tuple-element.26), channel_id=1, source_target_pairs={{0,32},{1,129},{2,34},{3,131},{4,36},{5,133},{6,38},{7,135},{8,40}... | collective-permute-start | bytes 786440 | tf_op jit(solution)/shard_map/ppermute | solution.py:29
  12.8 6.4 %collective-permute-start = (bf16[100,1024]{1,0:T(8,128)(2,1)S(1)}, bf16[100,1024]{1,0:T(8,128)(2,1)S(1)}, u32[]{:S(2)}, u32[]{:S(2)}) collective-permute-start(bf16[100,1024]{1,0:T(8,128)(2,1)S(1)} %get-tuple-element.17), channel_id=1, source_target_pairs={{0,31},{1,2},{2,1},{3,4},{4,3},{5,6},{6,5},{7,8},{8,7},{9,10},{10,... | collective-permute-start | bytes 614408 | tf_op jit(solution)/shard_map/ppermute | solution.py:52
  19.3 8.5 %collective-permute-start.1 = (bf16[100,1024]{1,0:T(8,128)(2,1)S(1)}, bf16[100,1024]{1,0:T(8,128)(2,1)S(1)}, u32[]{:S(2)}, u32[]{:S(2)}) collective-permute-start(bf16[100,1024]{1,0:T(8,128)(2,1)S(1)} %get-tuple-element.18), channel_id=1, source_target_pairs={{0,1},{1,0},{2,3},{3,2},{4,5},{5,4},{6,7},{7,6},{8,9},{9,8},{10,11... | collective-permute-start | bytes 614408 | tf_op jit(solution)/shard_map/ppermute | solution.py:29
  27.8 0.0 copy-done
  27.8 0.8 shard_map.87
  28.7 0.0 copy-start.1
  28.7 0.0 copy-start.2
  28.7 0.0 collective-permute-done.4
  28.7 0.0 collective-permute-done.5
  28.8 0.0 collective-permute-done.6
  28.8 3.8 %collective-permute-start.9 = (bf16[256,2048]{1,0:T(8,128)(2,1)S(1)}, bf16[256,2048]{1,0:T(8,128)(2,1)S(1)}, u32[]{:S(2)}, u32[]{:S(2)}) collective-permute-start(bf16[256,2048]{1,0:T(8,128)(2,1)S(1)} %constant_dynamic-update-slice_fusion.here), channel_id=1, source_target_pairs={{0,256},{1,65},{2,258},{3,67},{4,260},{5,69},{6,262},{7,71},{8,264... | collective-permute-start | bytes 3145736 | tf_op jit(solution)/shard_map/ppermute | solution.py:29
  32.6 3.1 %collective-permute-start.8 = (bf16[256,2048]{1,0:T(8,128)(2,1)S(1)}, bf16[256,2048]{1,0:T(8,128)(2,1)S(1)}, u32[]{:S(2)}, u32[]{:S(2)}) collective-permute-start(bf16[256,2048]{1,0:T(8,128)(2,1)S(1)} %constant_dynamic-update-slice_fusion.here), channel_id=1, source_target_pairs={{0,386},{1,97},{2,384},{3,99},{4,390},{5,101},{6,388},{7,103},{8,3... | collective-permute-start | bytes 3145736 | tf_op jit(solution)/shard_map/ppermute | solution.py:29
  35.6 2.2 %collective-permute-start.7 = (bf16[256,2048]{1,0:T(8,128)(2,1)S(1)}, bf16[256,2048]{1,0:T(8,128)(2,1)S(1)}, u32[]{:S(2)}, u32[]{:S(2)}) collective-permute-start(bf16[256,2048]{1,0:T(8,128)(2,1)S(1)} %constant_dynamic-update-slice_fusion.here), channel_id=1, source_target_pairs={{0,128},{1,33},{2,130},{3,35},{4,132},{5,37},{6,134},{7,39},{8,136... | collective-permute-start | bytes 3145736 | tf_op jit(solution)/shard_map/ppermute | solution.py:29
  37.9 0.0 collective-permute-done.near
  37.9 0.0 collective-permute-done.1.mate
  37.9 0.0 copy-done.1
  37.9 0.0 copy-done.2
  37.9 3.1 %shard_map.88 = (bf16[256,128]{1,0:T(8,128)(2,1)S(1)}, f32[6144,128]{1,0:T(8,128)S(1)}) custom-call(s32[32,128]{1,0:T(8,128)S(1)} %copy-done.2, bf16[32,16,128]{2,1,0:T(8,128)(2,1)S(1)} %copy-done.1, bf16[100,1024]{1,0:T(8,128)(2,1)S(1)} %collective-permute-done.near, bf16[100,1024]{1,0:T(8,128)(2,1)S(1)} %collective-permute-done.1.mate, ...), custom_call_target="tpu_custom_call" | custom-call | flops 3000000000 | bytes 1048576 | tf_op jit(solution)/shard_map/pallas_call | solution.py:326
  41.0 6.7 %collective-permute-start.2 = (bf16[256,128]{1,0:T(8,128)(2,1)S(1)}, bf16[256,128]{1,0:T(8,128)(2,1)S(1)}, u32[]{:S(2)}, u32[]{:S(2)}) collective-permute-start(bf16[256,128]{1,0:T(8,128)(2,1)S(1)} %get-tuple-element.21), channel_id=1, source_target_pairs={{0,31},{1,2},{2,1},{3,4},{4,3},{5,6},{6,5},{7,8},{8,7},{9,10},{10,... | collective-permute-start | bytes 196616 | tf_op jit(solution)/shard_map/ppermute | solution.py:52
  47.7 0.0 copy-start.3
  47.7 2.7 %shard_map.89 = bf16[256,128]{1,0:T(8,128)(2,1)S(1)} custom-call(s32[32,128]{1,0:T(8,128)S(1)} %copy-done.2, bf16[32,16,128]{2,1,0:T(8,128)(2,1)S(1)} %copy-done.1, f32[6144,128]{1,0:T(8,128)S(1)} %get-tuple-element.22.table), custom_call_target="tpu_custom_call" | custom-call | flops 3000000000 | bytes 1048576 | tf_op jit(solution)/shard_map/pallas_call | solution.py:330
  50.4 12.9 %collective-permute-done.2 = bf16[256,128]{1,0:T(8,128)(2,1)S(1)} collective-permute-done((bf16[256,128]{1,0:T(8,128)(2,1)S(1)}, bf16[256,128]{1,0:T(8,128)(2,1)S(1)}, u32[]{:S(2)}, u32[]{:S(2)}) %collective-permute-start.2) | collective-permute-done | bytes 65568 | tf_op jit(solution)/shard_map/ppermute | solution.py:52
  63.4 1.9 %collective-permute-start.3 = (bf16[768,128]{1,0:T(8,128)(2,1)S(1)}, bf16[768,128]{1,0:T(8,128)(2,1)S(1)}, u32[]{:S(2)}, u32[]{:S(2)}) collective-permute-start(bf16[768,128]{1,0:T(8,128)(2,1)S(1)} %pad_maximum_fusion.packed), channel_id=1, source_target_pairs={{0,1},{1,0},{2,3},{3,2},{4,5},{5,4},{6,7},{7,6},{8,9},{9,8},{10,11... | collective-permute-start | bytes 589832 | tf_op jit(solution)/shard_map/ppermute | solution.py:29
  65.3 0.0 copy-done.3
  65.3 0.8 shard_map.90
  66.1 0.6 collective-permute-done.3.mate
  66.7 1.5 %shard_map.91.rest = bf16[1024,1024]{1,0:T(8,128)(2,1)S(1)} custom-call(bf16[768,128]{1,0:T(8,128)(2,1)S(1)} %pad_maximum_fusion.packed, bf16[768,128]{1,0:T(8,128)(2,1)S(1)} %collective-permute-done.3.mate, bf16[128,1024]{1,0:T(8,128)(2,1)S(1)} %get-tuple-element.23.wide, f32[1,1024]{1,0:T(1,128)S(1)} %bitcast.5), custom_call_target="tpu_custom_call" | custom-call | flops 3000000000 | bytes 1048576 | tf_op jit(solution)/shard_map/pallas_call | solution.py:341
  68.2 0.0 collective-permute-done.9.across
  68.2 0.0 collective-permute-done.8.after
  68.2 0.0 collective-permute-done.7.before
  68.2 5.6 %shard_map.92 = (bf16[4,1024,128]{2,1,0:T(8,128)(2,1)S(1)}, bf16[4,1536,128]{2,1,0:T(8,128)(2,1)S(1)}, bf16[4,1536,128]{2,1,0:T(8,128)(2,1)S(1)}, bf16[8,512,128]{2,1,0:T(8,128)(2,1)S(1)}, bf16[512,1024]{1,0:T(8,128)(2,1)}) custom-call(bf16[512,1024]{1,0:T(8,128)(2,1)S(1)} %get-tuple-element.24.latent, bf16[512,1024]{1,0:T(8,128)(2,1)S(1)} %get-tuple-element.25.own, ...), custom_call_target="tpu_custom_call" | custom-call | flops 8000000000 | bytes 1048576 | tf_op jit(solution)/shard_map/pallas_call | solution.py:344
  73.8 5.1 %shard_map.94 = bf16[12,512,128]{2,1,0:T(8,128)(2,1)S(1)} custom-call(bf16[4,1024,128]{2,1,0:T(8,128)(2,1)S(1)} %get-tuple-element.28.q, bf16[4,1536,128]{2,1,0:T(8,128)(2,1)S(1)} %get-tuple-element.29.k, bf16[4,1536,128]{2,1,0:T(8,128)(2,1)S(1)} %get-tuple-element.30.v, bf16[8,512,128]{2,1,0:T(8,128)(2,1)S(1)} %get-tuple-element.31.refs_0_.my_cols), custom_call_target="tpu_custom_call" | custom-call | flops 8000000000 | bytes 1048576 | tf_op jit(solution)/shard_map/pallas_call | solution.py:357
  78.9 2.1 %collective-permute-start.10 = (bf16[12,512,128]{2,1,0:T(8,128)(2,1)S(1)}, bf16[12,512,128]{2,1,0:T(8,128)(2,1)S(1)}, u32[]{:S(2)}, u32[]{:S(2)}) collective-permute-start(bf16[12,512,128]{2,1,0:T(8,128)(2,1)S(1)} %shard_map.94), channel_id=1, source_target_pairs={{0,1},{1,0},{2,3},{3,2},{4,5},{5,4},{6,7},{7,6},{8,9},{9,8},{10,11... | collective-permute-start | bytes 4718600 | tf_op jit(solution)/shard_map/ppermute | solution.py:29
  81.0 5.1 %shard_map.93.mine = bf16[4,512,128]{2,1,0:T(8,128)(2,1)S(1)} custom-call(bf16[4,1024,128]{2,1,0:T(8,128)(2,1)S(1)} %get-tuple-element.28.q, bf16[4,1536,128]{2,1,0:T(8,128)(2,1)S(1)} %get-tuple-element.29.k, bf16[4,1536,128]{2,1,0:T(8,128)(2,1)S(1)} %get-tuple-element.30.v), custom_call_target="tpu_custom_call" | custom-call | flops 8000000000 | bytes 1048576 | tf_op jit(solution)/shard_map/pallas_call | solution.py:357
  86.0 0.0 collective-permute-done.10.theirs
  86.1 2.1 %shard_map.95 = bf16[512,1024]{1,0:T(8,128)(2,1)} custom-call(bf16[4,512,128]{2,1,0:T(8,128)(2,1)S(1)} %shard_map.93.mine, bf16[8,512,128]{2,1,0:T(8,128)(2,1)S(1)} %get-tuple-element.31.refs_0_.my_cols, bf16[12,512,128]{2,1,0:T(8,128)(2,1)S(1)} %collective-permute-done.10.theirs), custom_call_target="tpu_custom_call" | custom-call | flops 1000000000 | bytes 1048576 | tf_op jit(solution)/shard_map/pallas_call | solution.py:361
  (5 shorter events, 0.1 us)
Async XLA Ops:
  0.6 27.2 %copy-start = (bf16[100,1024]{1,0:T(8,128)(2,1)S(1)}, bf16[100,1024]{1,0:T(8,128)(2,1)}, u32[]{:S(2)}) copy-start(bf16[100,1024]{1,0:T(8,128)(2,1)} %w_in.1) | copy-start | bytes 614404
  2.3 26.5 %collective-permute-start.6 = (bf16[64,2048]{1,0:T(8,128)(2,1)S(1)}, bf16[64,2048]{1,0:T(8,128)(2,1)S(1)}, u32[]{:S(2)}, u32[]{:S(2)}) collective-permute-start(bf16[64,2048]{1,0:T(8,128)(2,1)S(1)} %get-tuple-element.26), channel_id=1, source_target_pairs={{0,64},{1,257},{2,66},{3,259},{4,68},{5,261},{6,70},{7,263},{8,72}... | collective-permute-start | bytes 786440 | tf_op jit(solution)/shard_map/ppermute | solution.py:29
  7.3 21.5 %collective-permute-start.5 = (bf16[64,2048]{1,0:T(8,128)(2,1)S(1)}, bf16[64,2048]{1,0:T(8,128)(2,1)S(1)}, u32[]{:S(2)}, u32[]{:S(2)}) collective-permute-start(bf16[64,2048]{1,0:T(8,128)(2,1)S(1)} %get-tuple-element.26), channel_id=1, source_target_pairs={{0,96},{1,387},{2,98},{3,385},{4,100},{5,391},{6,102},{7,389},{8,1... | collective-permute-start | bytes 786440 | tf_op jit(solution)/shard_map/ppermute | solution.py:29
  9.2 19.5 %collective-permute-start.4 = (bf16[64,2048]{1,0:T(8,128)(2,1)S(1)}, bf16[64,2048]{1,0:T(8,128)(2,1)S(1)}, u32[]{:S(2)}, u32[]{:S(2)}) collective-permute-start(bf16[64,2048]{1,0:T(8,128)(2,1)S(1)} %get-tuple-element.26), channel_id=1, source_target_pairs={{0,32},{1,129},{2,34},{3,131},{4,36},{5,133},{6,38},{7,135},{8,40}... | collective-permute-start | bytes 786440 | tf_op jit(solution)/shard_map/ppermute | solution.py:29
  12.8 25.0 %collective-permute-start = (bf16[100,1024]{1,0:T(8,128)(2,1)S(1)}, bf16[100,1024]{1,0:T(8,128)(2,1)S(1)}, u32[]{:S(2)}, u32[]{:S(2)}) collective-permute-start(bf16[100,1024]{1,0:T(8,128)(2,1)S(1)} %get-tuple-element.17), channel_id=1, source_target_pairs={{0,31},{1,2},{2,1},{3,4},{4,3},{5,6},{6,5},{7,8},{8,7},{9,10},{10,... | collective-permute-start | bytes 614408 | tf_op jit(solution)/shard_map/ppermute | solution.py:52
  19.3 18.6 %collective-permute-start.1 = (bf16[100,1024]{1,0:T(8,128)(2,1)S(1)}, bf16[100,1024]{1,0:T(8,128)(2,1)S(1)}, u32[]{:S(2)}, u32[]{:S(2)}) collective-permute-start(bf16[100,1024]{1,0:T(8,128)(2,1)S(1)} %get-tuple-element.18), channel_id=1, source_target_pairs={{0,1},{1,0},{2,3},{3,2},{4,5},{5,4},{6,7},{7,6},{8,9},{9,8},{10,11... | collective-permute-start | bytes 614408 | tf_op jit(solution)/shard_map/ppermute | solution.py:29
  28.7 9.2 %copy-start.1 = (bf16[32,16,128]{2,1,0:T(8,128)(2,1)S(1)}, bf16[32,16,128]{2,1,0:T(8,128)(2,1)}, u32[]{:S(2)}) copy-start(bf16[32,16,128]{2,1,0:T(8,128)(2,1)} %weight.3) | copy-start | bytes 393220
  28.7 9.2 %copy-start.2 = (s32[32,128]{1,0:T(8,128)S(1)}, s32[32,128]{1,0:T(8,128)}, u32[]{:S(2)}) copy-start(s32[32,128]{1,0:T(8,128)} %index.3) | copy-start | bytes 49156
  28.8 39.4 %collective-permute-start.9 = (bf16[256,2048]{1,0:T(8,128)(2,1)S(1)}, bf16[256,2048]{1,0:T(8,128)(2,1)S(1)}, u32[]{:S(2)}, u32[]{:S(2)}) collective-permute-start(bf16[256,2048]{1,0:T(8,128)(2,1)S(1)} %constant_dynamic-update-slice_fusion.here), channel_id=1, source_target_pairs={{0,256},{1,65},{2,258},{3,67},{4,260},{5,69},{6,262},{7,71},{8,264... | collective-permute-start | bytes 3145736 | tf_op jit(solution)/shard_map/ppermute | solution.py:29
  32.6 35.6 %collective-permute-start.8 = (bf16[256,2048]{1,0:T(8,128)(2,1)S(1)}, bf16[256,2048]{1,0:T(8,128)(2,1)S(1)}, u32[]{:S(2)}, u32[]{:S(2)}) collective-permute-start(bf16[256,2048]{1,0:T(8,128)(2,1)S(1)} %constant_dynamic-update-slice_fusion.here), channel_id=1, source_target_pairs={{0,386},{1,97},{2,384},{3,99},{4,390},{5,101},{6,388},{7,103},{8,3... | collective-permute-start | bytes 3145736 | tf_op jit(solution)/shard_map/ppermute | solution.py:29
  35.6 32.6 %collective-permute-start.7 = (bf16[256,2048]{1,0:T(8,128)(2,1)S(1)}, bf16[256,2048]{1,0:T(8,128)(2,1)S(1)}, u32[]{:S(2)}, u32[]{:S(2)}) collective-permute-start(bf16[256,2048]{1,0:T(8,128)(2,1)S(1)} %constant_dynamic-update-slice_fusion.here), channel_id=1, source_target_pairs={{0,128},{1,33},{2,130},{3,35},{4,132},{5,37},{6,134},{7,39},{8,136... | collective-permute-start | bytes 3145736 | tf_op jit(solution)/shard_map/ppermute | solution.py:29
  41.0 22.4 %collective-permute-start.2 = (bf16[256,128]{1,0:T(8,128)(2,1)S(1)}, bf16[256,128]{1,0:T(8,128)(2,1)S(1)}, u32[]{:S(2)}, u32[]{:S(2)}) collective-permute-start(bf16[256,128]{1,0:T(8,128)(2,1)S(1)} %get-tuple-element.21), channel_id=1, source_target_pairs={{0,31},{1,2},{2,1},{3,4},{4,3},{5,6},{6,5},{7,8},{8,7},{9,10},{10,... | collective-permute-start | bytes 196616 | tf_op jit(solution)/shard_map/ppermute | solution.py:52
  47.7 17.6 %copy-start.3 = (f32[1024]{0:T(1024)S(1)}, f32[1024]{0:T(1024)}, u32[]{:S(2)}) copy-start(f32[1024]{0:T(1024)} %param.11) | copy-start | bytes 12292
  63.4 3.3 %collective-permute-start.3 = (bf16[768,128]{1,0:T(8,128)(2,1)S(1)}, bf16[768,128]{1,0:T(8,128)(2,1)S(1)}, u32[]{:S(2)}, u32[]{:S(2)}) collective-permute-start(bf16[768,128]{1,0:T(8,128)(2,1)S(1)} %pad_maximum_fusion.packed), channel_id=1, source_target_pairs={{0,1},{1,0},{2,3},{3,2},{4,5},{5,4},{6,7},{7,6},{8,9},{9,8},{10,11... | collective-permute-start | bytes 589832 | tf_op jit(solution)/shard_map/ppermute | solution.py:29
  78.9 7.1 %collective-permute-start.10 = (bf16[12,512,128]{2,1,0:T(8,128)(2,1)S(1)}, bf16[12,512,128]{2,1,0:T(8,128)(2,1)S(1)}, u32[]{:S(2)}, u32[]{:S(2)}) collective-permute-start(bf16[12,512,128]{2,1,0:T(8,128)(2,1)S(1)} %shard_map.94), channel_id=1, source_target_pairs={{0,1},{1,0},{2,3},{3,2},{4,5},{5,4},{6,7},{7,6},{8,9},{9,8},{10,11... | collective-permute-start | bytes 4718600 | tf_op jit(solution)/shard_map/ppermute | solution.py:29

commit v4 on v3

--- a/solution.py
+++ b/solution.py
@@ -113,7 +113,11 @@
         copy.wait()
 
 
-def table_kernel(cells, w_in, table, wide, tall):
+def sources_of(i):
+    return jnp.where(i == 0, 0, jnp.where(i == 1, 3, i - 1))
+
+
+def table_kernel(cells, w_in, gain, table, wide, mixed, mixed_gain, tall):
     wide[96:, :] = jnp.zeros((32, 1024), BF)
     wide[:100, :] = w_in[...]
     tall[96:, :] = jnp.zeros((32, 1024), F32)
@@ -124,6 +128,29 @@
         return carry
 
     lax.fori_loop(0, 4, part, 0)
+
+    core, dp = core_index(), lax.axis_index("dp")
+    x, y = lax.rem(dp, 4), lax.div(dp, 4)
+    place = lax.broadcasted_iota(jnp.int32, (256, 1024), 1)
+    group, member = sources_of(place >> 8), sources_of((place >> 6) & 3)
+    row = (y + jnp.where(core == 0, group, member)) & 3
+    column = (x + jnp.where(core == 0, member, group)) & 3
+    source = row * 256 + column * 64 + (place & 63)
+    high = gain[...].astype(BF).astype(F32)
+    middle = (gain[...] - high).astype(BF).astype(F32)
+    low = gain[...] - high - middle
+    line = lax.broadcasted_iota(jnp.int32, (16, 1024), 0)
+    parts = jnp.where(line == 0, high, jnp.where(line == 1, middle, jnp.where(line == 2, low, 0.0)))
+    parts = parts.astype(BF)
+    total, total_gain = None, None
+    for i in range(0, 1024, 256):
+        here = lax.broadcasted_iota(jnp.int32, (256, 1024), 0) + i
+        move = jnp.where(here == source, 1.0, 0.0).astype(BF)
+        one, two_ = dot(wide[:, i : i + 256], move), dot(parts[:, i : i + 256], move)
+        total = one if i == 0 else total + one
+        total_gain = two_ if i == 0 else total_gain + two_
+    mixed[...] = total.astype(BF)
+    mixed_gain[...] = jnp.sum(total_gain, axis=0, keepdims=True)
 
 
 def encode_blocks(start, index, weight, table, out, picked):
@@ -160,23 +187,22 @@
     average = jnp.mean(embedded, axis=1, keepdims=True)
     centered = embedded - average
     spread = jnp.mean(centered * centered, axis=1, keepdims=True)
-    return embedded, (centered * lax.rsqrt(spread + 1e-05) * gain).astype(BF)
-
-
-def embed_own_kernel(packed, wide, gain, normed, latent):
+    return (centered * lax.rsqrt(spread + 1e-05) * gain).astype(BF)
+
+
+def embed_own_kernel(packed, wide, mixed, gain, normed, latent):
     at = core_index() * 256
     for row, start in ((0, at), (256, 256 - at)):
-        embedded, unit = normalised(packed[row : row + 256, :], wide[...], gain[...])
-        normed[rows_at(start), :] = unit
-        latent[rows_at(start), :] = embedded.astype(BF)
-
-
-def embed_rest_kernel(packed, mate, wide, gain, normed):
+        piece = packed[row : row + 256, :]
+        normed[rows_at(start), :] = normalised(piece, mixed[...], gain[...])
+        latent[rows_at(start), :] = dot(piece, wide[...]).astype(BF)
+
+
+def embed_rest_kernel(packed, mate, mixed, gain, normed):
     at = core_index() * 256
     pieces = ((mate, 0, 256 - at), (mate, 256, at), (mate, 512, 512), (packed, 512, 768))
     for piece, row, start in pieces:
-        _, unit = normalised(piece[row : row + 256, :], wide[...], gain[...])
-        normed[rows_at(start), :] = unit
+        normed[rows_at(start), :] = normalised(piece[row : row + 256, :], mixed[...], gain[...])
 
 
 def head_ones():
@@ -200,50 +226,62 @@
         ref[p, at, :] = rows[:, p * 128 : (p + 1) * 128]
 
 
-def project_kernel(
-    latent, own, rest, here, before, after, across, q, k, v, out_cols, latent_out, weights, sem
-):
+def first_kernel(latent, own, rest, here, before, after, mine, mates, sides, latent_out, sem):
     copy = pltpu.make_async_copy(latent, latent_out, sem)
     copy.start()
+    for rows, sums, skip in ((own[...], mine, 0), (rest[:512, :], mates, 0), (rest[512:, :], sides, 512)):
+        for col in range(skip, 1536, 512):
+            cols = slice(col, col + 512)
+            weights = jnp.concatenate([here[:, cols], before[:, cols], after[:, cols]], axis=0)
+            sums[:, col - skip : col - skip + 512] = dot(rows[:, :768], weights)
+    copy.wait()
+
+
+def project_kernel(own, rest, across, mine, mates, sides, q, k, v):
     core = core_index()
-    dp = lax.axis_index("dp")
+    ones = head_ones()
+
+    def whole(rows, sums, skip, col):
+        return sums[:, col - skip : col - skip + 512] + dot(rows, across[:, col : col + 512])
+
+    for rows, sums, start in (
+        (own[:, 768:], mine, core * 512),
+        (rest[:512, 768:], mates, 512 - core * 512),
+    ):
+        at = rows_at(start + 256, 512)
+        put_heads(k, at, unit_heads(whole(rows, sums, 0, 512), ones))
+        put_heads(q, rows_at(start, 512), unit_heads(whole(rows, sums, 0, 0), ones))
+        put_heads(v, at, whole(rows, sums, 0, 1024).astype(BF))
+    far, near = rows_at(1280 - core * 1280), rows_at(core * 1280)
+    rows = rest[512:, 768:]
+    for ref, part in (
+        (k, unit_heads(whole(rows, sides, 512, 512), ones)),
+        (v, whole(rows, sides, 512, 1024).astype(BF)),
+    ):
+        put_heads(ref, far, part[:256])
+        put_heads(ref, near, part[256:])
+
+
+def place_columns(pieces, out):
+    core, dp = core_index(), lax.axis_index("dp")
     x, y = lax.rem(dp, 4), lax.div(dp, 4)
     first, second = jnp.where(core == 0, x, y), jnp.where(core == 0, y, x)
-    for step, piece in zip(SOURCES, (here, before, after, across)):
+    for step, piece in zip(SOURCES, pieces):
         other = lax.rem(second + step, 4)
         for m in range(4):
             mine = lax.rem(first + SOURCES[m], 4)
             block = jnp.where(core == 0, other * 4 + mine, mine * 4 + other)
-            rows = slice(m * 64, m * 64 + 64)
-            weights[pl.ds(pl.multiple_of(block * 64, 64), 64), :] = piece[rows, :1536]
             half = lax.div(block, 8)
             at = pl.ds(pl.multiple_of(block * 64 - half * 512, 64), 64)
             for j in range(4):
-                out_cols[half * 4 + j, at, :] = piece[rows, 1536 + j * 128 : 1664 + j * 128]
-    ones = head_ones()
-    for rows, start in ((own, core * 512), (rest, 512 - core * 512)):
-        rows = rows[:512, :]
-        at = rows_at(start + 256, 512)
-        put_heads(k, at, unit_heads(dot(rows, weights[:, 512:1024]), ones))
-        put_heads(q, rows_at(start, 512), unit_heads(dot(rows, weights[:, :512]), ones))
-        put_heads(v, at, dot(rows, weights[:, 1024:]).astype(BF))
-    far, near = rows_at(1280 - core * 1280), rows_at(core * 1280)
-    rows = rest[512:, :]
-    for ref, part in (
-        (k, unit_heads(dot(rows, weights[:, 512:1024]), ones)),
-        (v, dot(rows, weights[:, 1024:]).astype(BF)),
-    ):
-        put_heads(ref, far, part[:256])
-        put_heads(ref, near, part[256:])
-    copy.wait()
+                cols = slice(1536 + j * 128, 1664 + j * 128)
+                out[4 + half * 4 + j, at, :] = piece[m * 64 : m * 64 + 64, cols]
 
 
 def attend_kernel(other, q, k, v, *refs):
+    *pieces, out = refs
     if other:
-        cols, out = refs
-        out[4:, :, :] = cols[...]
-    else:
-        (out,) = refs
+        place_columns(pieces, out)
     core = core_index()
     shard = 1 - core if other else core
     scale = math.log2(math.e) / 8.0
@@ -273,7 +311,7 @@
     lax.fori_loop(0, 4, tile, 0)
 
 
-def out_kernel(mine, my_cols, theirs, update, done, sem):
+def out_kernel(mine, sent, theirs, update, done, sem):
     core = core_index()
 
     def join(ref, first, rows):
@@ -286,9 +324,9 @@
     for i in range(2):
         rows = slice(i * 256, i * 256 + 256)
         here, there = join(mine, 0, rows), join(theirs, 0, rows)
-        for ref, skip, at in ((my_cols, 0, near), (theirs, 4, far)):
-            top = join(ref, skip + core * 4, every)
-            low = join(ref, skip + 4 - core * 4, every)
+        for ref, at in ((sent, near), (theirs, far)):
+            top = join(ref, 4 + core * 4, every)
+            low = join(ref, 8 - core * 4, every)
             done[rows, at] = (dot(here, top) + dot(there, low)).astype(BF)
         copies.append(pltpu.make_async_copy(done.at[rows], update.at[rows], sem.at[i]))
         copies[i].start()
@@ -319,9 +357,15 @@
         gathered.append(send(group, along(False, shift)))
 
     grown, tall = ((6144, 128), F32), ((128, 1024), F32)
-    table, wide = call(
-        table_kernel, [((4096, 128), F32), ((128, 1024), BF)], [tall], 2_000_000_000, 8, 2
-    )(cells, w_in)
+    spread = ((128, 1024), BF)
+    table, wide, mixed, gain = call(
+        table_kernel,
+        [((4096, 128), F32), spread, spread, ((1, 1024), F32)],
+        [tall],
+        2_000_000_000,
+        12,
+        3,
+    )(cells, w_in, ln_gain[None])
     picked = ((16, 128, 128), F32)
     edge, table = call(
         encode_edge_kernel, [((256, 128), BF), grown], [tall, picked], 3_000_000_000, 8, 4, 1
@@ -333,30 +377,33 @@
     packed = jnp.concatenate([edge, inner, near], axis=0)
     mate = swap(packed)
 
-    gain = ln_gain[None]
     tile = ((512, 1024), BF)
-    own_normed, latent = call(
-        embed_own_kernel, [tile, tile], [], 1_500_000_000, 12, 3
-    )(packed, wide, gain)
-    (rest_normed,) = call(
+    own, latent = call(embed_own_kernel, [tile, tile], [], 1_500_000_000, 12, 4)(
+        packed, wide, mixed, gain
+    )
+    (rest,) = call(
         embed_rest_kernel, [((1024, 1024), BF)], [], 3_000_000_000, 12, 4
-    )(packed, mate, wide, gain)
-    q, k, v, my_cols, latent = call(
-        project_kernel,
-        [((4, n, 128), BF) for n in (1024, 1536, 1536)] + [((8, 512, 128), BF), tile],
-        [((1024, 1536), BF), pltpu.SemaphoreType.DMA],
-        8_000_000_000,
-        16,
-        7,
-        any_out=(4,),
-    )(latent, own_normed, rest_normed, *gathered)
+    )(packed, mate, mixed, gain)
+    *sums, latent = call(
+        first_kernel,
+        [((512, 1536), F32), ((512, 1536), F32), ((512, 1024), F32), tile],
+        [pltpu.SemaphoreType.DMA],
+        6_000_000_000,
+        12,
+        6,
+        any_out=(3,),
+    )(latent, own, rest, *gathered[:3])
+    q, k, v = call(
+        project_kernel, [((4, n, 128), BF) for n in (1024, 1536, 1536)], [], 3_000_000_000, 12, 6
+    )(own, rest, gathered[3], *sums)
 
     def attend(other, *args):
         kernel = functools.partial(attend_kernel, other)
         outs = [((12 if other else 4, 512, 128), BF)]
         return call(kernel, outs, [], 8_000_000_000, 16, len(args))(*args)[0]
 
-    theirs = swap(attend(True, q, k, v, my_cols))
+    sent = attend(True, q, k, v, *gathered)
+    theirs = swap(sent)
     mine = attend(False, q, k, v)
     (update,) = call(
         out_kernel,
@@ -366,7 +413,7 @@
         12,
         3,
         any_out=(0,),
-    )(mine, my_cols, theirs)
+    )(mine, sent, theirs)
     return latent[None], update[None]
 
 

time: 88.6 us -> 86.9 us (0.981)
  the two profiles are of different devices: /device:TPU:11 before, /device:TPU:33 now
where the time goes in v4:
time: 86.9 us; the launch traced here: 86.4 us
  starting transfers between devices  48.2 us (55%)
  Pallas kernels  30 us (35%)
  waiting for transfers between devices  5.57 us (6%)
  local copies, waits for them, and re-layouts  1.7 us (2%)
  between operations  0.9 us (1%)
    ppermute x9, starting transfers between devices, send(): return lax.ppermute(array, AXES, pairs)  33 us
    ppermute x2, starting transfers between devices, ring(): return lax.ppermute(array, 'space', [(s, move(s) % 32) for s in range(32)])  15.2 us
    pallas_call x2, Pallas kernels, attend(): return call(kernel, outs, [], 8000000000, 16, len(args))(*args)[0]  10.4 us
    ppermute x2, waiting for transfers between devices, ring(): return lax.ppermute(array, 'space', [(s, move(s) % 32) for s in range(32)])  4.56 us
    pallas_call x1, Pallas kernels, shards(): call(first_kernel, [((512, 1536), F32), ((512, 1536), F32), ((512, 1024),...  4.05 us
    pallas_call x1, Pallas kernels, shards(): call(encode_edge_kernel, [((256, 128), BF), grown], [tall, picked], 30000...  3.07 us
    pallas_call x1, Pallas kernels, shards(): call(encode_inner_kernel, [((256, 128), BF)], [picked], 3000000000, 8, 2, 1)  2.72 us
    pallas_call x1, Pallas kernels, shards(): call(out_kernel, [tile], [tile, pltpu.SemaphoreType.DMA((2,))], 100000000...  2.08 us
  transfers between devices with their start and end apart: 11, of which 3 were waited for; matrix products, arithmetic and copies ran while one was open for 0% of the time, Pallas kernels for 22%

profile of v4, /device:TPU:33, one launch (start us, length us, event | category | flops | bytes accessed | tf_op | source)
XLA Modules:
  0.0 86.4 jit_solution(17649931657623626037)
XLA Ops:
  0.6 1.6 %shard_map.86 = (bf16[64,2048]{1,0:T(8,128)(2,1)S(1)}, bf16[100,1024]{1,0:T(8,128)(2,1)S(1)}, bf16[100,1024]{1,0:T(8,128)(2,1)S(1)}, bf16[100,4096]{1,0:T(8,128)(2,1)S(1)}) custom-call(bf16[100,4096]{1,0:T(8,128)(2,1)} %bitcast.6, bf16[64,3072]{1,0:T(8,128)(2,1)} %w_qkv.1, bf16[64,1024]{1,0:T(8,128)(2,1)} %w_out.1), custom_call_target="tpu_custom_call" | custom-call | flops 100000000 | bytes 1048576 | tf_op jit(solution)/shard_map/pallas_call | solution.py:339
  2.2 2.4 %collective-permute-start.6 = (bf16[64,2048]{1,0:T(8,128)(2,1)S(1)}, bf16[64,2048]{1,0:T(8,128)(2,1)S(1)}, u32[]{:S(2)}, u32[]{:S(2)}) collective-permute-start(bf16[64,2048]{1,0:T(8,128)(2,1)S(1)} %get-tuple-element.32), channel_id=1, source_target_pairs={{0,64},{1,257},{2,66},{3,259},{4,68},{5,261},{6,70},{7,263},{8,72}... | collective-permute-start | bytes 786440 | tf_op jit(solution)/shard_map/ppermute | solution.py:29
  4.7 1.9 %collective-permute-start.5 = (bf16[64,2048]{1,0:T(8,128)(2,1)S(1)}, bf16[64,2048]{1,0:T(8,128)(2,1)S(1)}, u32[]{:S(2)}, u32[]{:S(2)}) collective-permute-start(bf16[64,2048]{1,0:T(8,128)(2,1)S(1)} %get-tuple-element.32), channel_id=1, source_target_pairs={{0,96},{1,387},{2,98},{3,385},{4,100},{5,391},{6,102},{7,389},{8,1... | collective-permute-start | bytes 786440 | tf_op jit(solution)/shard_map/ppermute | solution.py:29
  6.6 3.4 %collective-permute-start.4 = (bf16[64,2048]{1,0:T(8,128)(2,1)S(1)}, bf16[64,2048]{1,0:T(8,128)(2,1)S(1)}, u32[]{:S(2)}, u32[]{:S(2)}) collective-permute-start(bf16[64,2048]{1,0:T(8,128)(2,1)S(1)} %get-tuple-element.32), channel_id=1, source_target_pairs={{0,32},{1,129},{2,34},{3,131},{4,36},{5,133},{6,38},{7,135},{8,40}... | collective-permute-start | bytes 786440 | tf_op jit(solution)/shard_map/ppermute | solution.py:29
  9.9 7.2 %collective-permute-start = (bf16[100,1024]{1,0:T(8,128)(2,1)S(1)}, bf16[100,1024]{1,0:T(8,128)(2,1)S(1)}, u32[]{:S(2)}, u32[]{:S(2)}) collective-permute-start(bf16[100,1024]{1,0:T(8,128)(2,1)S(1)} %get-tuple-element.21), channel_id=1, source_target_pairs={{0,31},{1,2},{2,1},{3,4},{4,3},{5,6},{6,5},{7,8},{8,7},{9,10},{10,... | collective-permute-start | bytes 614408 | tf_op jit(solution)/shard_map/ppermute | solution.py:52
  17.1 1.9 %collective-permute-start.1 = (bf16[100,1024]{1,0:T(8,128)(2,1)S(1)}, bf16[100,1024]{1,0:T(8,128)(2,1)S(1)}, u32[]{:S(2)}, u32[]{:S(2)}) collective-permute-start(bf16[100,1024]{1,0:T(8,128)(2,1)S(1)} %get-tuple-element.22), channel_id=1, source_target_pairs={{0,1},{1,0},{2,3},{3,2},{4,5},{5,4},{6,7},{7,6},{8,9},{9,8},{10,11... | collective-permute-start | bytes 614408 | tf_op jit(solution)/shard_map/ppermute | solution.py:29
  19.1 0.0 copy-start
  19.1 0.9 %copy-done = bf16[100,1024]{1,0:T(8,128)(2,1)S(1)} copy-done((bf16[100,1024]{1,0:T(8,128)(2,1)S(1)}, bf16[100,1024]{1,0:T(8,128)(2,1)}, u32[]{:S(2)}) %copy-start) | copy-done | bytes 204824
  20.0 0.0 copy-start.3
  20.0 0.7 copy-done.3
  20.7 0.0 copy-start.1
  20.7 0.0 copy-start.2
  20.7 1.7 %shard_map.87 = (f32[4096,128]{1,0:T(8,128)S(1)}, bf16[128,1024]{1,0:T(8,128)(2,1)S(1)}, bf16[128,1024]{1,0:T(8,128)(2,1)S(1)}, f32[1,1024]{1,0:T(1,128)S(1)}) custom-call(bf16[100,4096]{1,0:T(8,128)(2,1)S(1)} %get-tuple-element.23.cells, bf16[100,1024]{1,0:T(8,128)(2,1)S(1)} %copy-done, f32[1,1024]{1,0:T(1,128)S(1)} %bitcast.4), custom_call_target="tpu_custom_call" | custom-call | flops 2000000000 | bytes 1048576 | tf_op jit(solution)/shard_map/pallas_call | solution.py:361
  22.4 0.0 collective-permute-done.4
  22.4 0.0 collective-permute-done.5
  22.5 0.0 collective-permute-done.6
  22.5 4.0 %collective-permute-start.8 = (bf16[256,2048]{1,0:T(8,128)(2,1)S(1)}, bf16[256,2048]{1,0:T(8,128)(2,1)S(1)}, u32[]{:S(2)}, u32[]{:S(2)}) collective-permute-start(bf16[256,2048]{1,0:T(8,128)(2,1)S(1)} %constant_dynamic-update-slice_fusion.here.refs_0_), channel_id=1, source_target_pairs={{0,386},{1,97},{2,384},{3,99},{4,390},{5,101},{6,388},{7,103},{8,3... | collective-permute-start | bytes 3145736 | tf_op jit(solution)/shard_map/ppermute | solution.py:29
  26.5 1.9 %collective-permute-start.7 = (bf16[256,2048]{1,0:T(8,128)(2,1)S(1)}, bf16[256,2048]{1,0:T(8,128)(2,1)S(1)}, u32[]{:S(2)}, u32[]{:S(2)}) collective-permute-start(bf16[256,2048]{1,0:T(8,128)(2,1)S(1)} %constant_dynamic-update-slice_fusion.here.refs_0_), channel_id=1, source_target_pairs={{0,128},{1,33},{2,130},{3,35},{4,132},{5,37},{6,134},{7,39},{8,136... | collective-permute-start | bytes 3145736 | tf_op jit(solution)/shard_map/ppermute | solution.py:29
  28.4 0.0 collective-permute-done.near
  28.4 0.0 collective-permute-done.1.mate
  28.5 0.0 copy-done.1
  28.5 0.0 copy-done.2
  28.5 3.1 %shard_map.88 = (bf16[256,128]{1,0:T(8,128)(2,1)S(1)}, f32[6144,128]{1,0:T(8,128)S(1)}) custom-call(s32[32,128]{1,0:T(8,128)S(1)} %copy-done.2, bf16[32,16,128]{2,1,0:T(8,128)(2,1)S(1)} %copy-done.1, bf16[100,1024]{1,0:T(8,128)(2,1)S(1)} %collective-permute-done.near, bf16[100,1024]{1,0:T(8,128)(2,1)S(1)} %collective-permute-done.1.mate, ...), custom_call_target="tpu_custom_call" | custom-call | flops 3000000000 | bytes 1048576 | tf_op jit(solution)/shard_map/pallas_call | solution.py:370
  31.6 8.0 %collective-permute-start.2 = (bf16[256,128]{1,0:T(8,128)(2,1)S(1)}, bf16[256,128]{1,0:T(8,128)(2,1)S(1)}, u32[]{:S(2)}, u32[]{:S(2)}) collective-permute-start(bf16[256,128]{1,0:T(8,128)(2,1)S(1)} %get-tuple-element.25), channel_id=1, source_target_pairs={{0,31},{1,2},{2,1},{3,4},{4,3},{5,6},{6,5},{7,8},{8,7},{9,10},{10,... | collective-permute-start | bytes 196616 | tf_op jit(solution)/shard_map/ppermute | solution.py:52
  39.6 2.7 %shard_map.89 = bf16[256,128]{1,0:T(8,128)(2,1)S(1)} custom-call(s32[32,128]{1,0:T(8,128)S(1)} %copy-done.2, bf16[32,16,128]{2,1,0:T(8,128)(2,1)S(1)} %copy-done.1, f32[6144,128]{1,0:T(8,128)S(1)} %get-tuple-element.26.table), custom_call_target="tpu_custom_call" | custom-call | flops 3000000000 | bytes 1048576 | tf_op jit(solution)/shard_map/pallas_call | solution.py:374
  42.3 2.3 %collective-permute-start.9 = (bf16[256,2048]{1,0:T(8,128)(2,1)S(1)}, bf16[256,2048]{1,0:T(8,128)(2,1)S(1)}, u32[]{:S(2)}, u32[]{:S(2)}) collective-permute-start(bf16[256,2048]{1,0:T(8,128)(2,1)S(1)} %constant_dynamic-update-slice_fusion.here.refs_0_), channel_id=1, source_target_pairs={{0,256},{1,65},{2,258},{3,67},{4,260},{5,69},{6,262},{7,71},{8,264... | collective-permute-start | bytes 3145736 | tf_op jit(solution)/shard_map/ppermute | solution.py:29
  44.6 4.6 %collective-permute-done.2 = bf16[256,128]{1,0:T(8,128)(2,1)S(1)} collective-permute-done((bf16[256,128]{1,0:T(8,128)(2,1)S(1)}, bf16[256,128]{1,0:T(8,128)(2,1)S(1)}, u32[]{:S(2)}, u32[]{:S(2)}) %collective-permute-start.2) | collective-permute-done | bytes 65568 | tf_op jit(solution)/shard_map/ppermute | solution.py:52
  49.2 3.0 %collective-permute-start.3 = (bf16[768,128]{1,0:T(8,128)(2,1)S(1)}, bf16[768,128]{1,0:T(8,128)(2,1)S(1)}, u32[]{:S(2)}, u32[]{:S(2)}) collective-permute-start(bf16[768,128]{1,0:T(8,128)(2,1)S(1)} %pad_maximum_fusion.packed), channel_id=1, source_target_pairs={{0,1},{1,0},{2,3},{3,2},{4,5},{5,4},{6,7},{7,6},{8,9},{9,8},{10,11... | collective-permute-start | bytes 589832 | tf_op jit(solution)/shard_map/ppermute | solution.py:29
  52.2 0.9 %shard_map.90 = (bf16[512,1024]{1,0:T(8,128)(2,1)S(1)}, bf16[512,1024]{1,0:T(8,128)(2,1)S(1)}) custom-call(bf16[768,128]{1,0:T(8,128)(2,1)S(1)} %pad_maximum_fusion.packed, bf16[128,1024]{1,0:T(8,128)(2,1)S(1)} %get-tuple-element.27.wide, bf16[128,1024]{1,0:T(8,128)(2,1)S(1)} %get-tuple-element.28.mixed, f32[1,1024]{1,0:T(1,128)S(1)} %get-tuple-element.29.gain), custom_call_target="tpu_custom_call" | custom-call | flops 1500000000 | bytes 1048576 | tf_op jit(solution)/shard_map/pallas_call | solution.py:381
  53.1 0.1 collective-permute-done.3.mate
  53.2 1.5 %shard_map.91.rest = bf16[1024,1024]{1,0:T(8,128)(2,1)S(1)} custom-call(bf16[768,128]{1,0:T(8,128)(2,1)S(1)} %pad_maximum_fusion.packed, bf16[768,128]{1,0:T(8,128)(2,1)S(1)} %collective-permute-done.3.mate, bf16[128,1024]{1,0:T(8,128)(2,1)S(1)} %get-tuple-element.28.mixed, f32[1,1024]{1,0:T(1,128)S(1)} %get-tuple-element.29.gain), custom_call_target="tpu_custom_call" | custom-call | flops 3000000000 | bytes 1048576 | tf_op jit(solution)/shard_map/pallas_call | solution.py:384
  54.7 0.0 collective-permute-done.8.after.refs_2_
  54.7 0.0 collective-permute-done.7.before.refs_1_
  54.7 4.0 %shard_map.92 = (f32[512,1536]{1,0:T(8,128)S(1)}, f32[512,1536]{1,0:T(8,128)S(1)}, f32[512,1024]{1,0:T(8,128)S(1)}, bf16[512,1024]{1,0:T(8,128)(2,1)}) custom-call(bf16[512,1024]{1,0:T(8,128)(2,1)S(1)} %get-tuple-element.30.latent, bf16[512,1024]{1,0:T(8,128)(2,1)S(1)} %get-tuple-element.31.own, bf16[1024,1024]{1,0:T(8,128)(2,1)S(1)} %shard_map.91.rest, ...), custom_call_target="tpu_custom_call" | custom-call | flops 6000000000 | bytes 1048576 | tf_op jit(solution)/shard_map/pallas_call | solution.py:387
  58.8 0.9 %collective-permute-done.9.across.refs_3_ = bf16[256,2048]{1,0:T(8,128)(2,1)S(1)} collective-permute-done((bf16[256,2048]{1,0:T(8,128)(2,1)S(1)}, bf16[256,2048]{1,0:T(8,128)(2,1)S(1)}, u32[]{:S(2)}, u32[]{:S(2)}) %collective-permute-start.9) | collective-permute-done | bytes 1048608 | tf_op jit(solution)/shard_map/ppermute | solution.py:29
  59.6 2.1 %shard_map.93 = (bf16[4,1024,128]{2,1,0:T(8,128)(2,1)S(1)}, bf16[4,1536,128]{2,1,0:T(8,128)(2,1)S(1)}, bf16[4,1536,128]{2,1,0:T(8,128)(2,1)S(1)}) custom-call(bf16[512,1024]{1,0:T(8,128)(2,1)S(1)} %get-tuple-element.31.own, bf16[1024,1024]{1,0:T(8,128)(2,1)S(1)} %shard_map.91.rest, bf16[256,2048]{1,0:T(8,128)(2,1)S(1)} %collective-permute-done.9.across.refs_3_, ...), custom_call_target="tpu_custom_call" | custom-call | flops 3000000000 | bytes 1048576 | tf_op jit(solution)/shard_map/pallas_call | solution.py:396
  61.7 5.3 %shard_map.95.sent = bf16[12,512,128]{2,1,0:T(8,128)(2,1)S(1)} custom-call(bf16[4,1024,128]{2,1,0:T(8,128)(2,1)S(1)} %get-tuple-element.37.q, bf16[4,1536,128]{2,1,0:T(8,128)(2,1)S(1)} %get-tuple-element.38.k, bf16[4,1536,128]{2,1,0:T(8,128)(2,1)S(1)} %get-tuple-element.39.v, bf16[256,2048]{1,0:T(8,128)(2,1)S(1)} %constant_dynamic-update-slice_fusion.here.refs_0_, ...), custom_call_target="tpu_custom_call" | custom-call | flops 8000000000 | bytes 1048576 | tf_op jit(solution)/shard_map/pallas_call | solution.py:403
  67.1 12.2 %collective-permute-start.10 = (bf16[12,512,128]{2,1,0:T(8,128)(2,1)S(1)}, bf16[12,512,128]{2,1,0:T(8,128)(2,1)S(1)}, u32[]{:S(2)}, u32[]{:S(2)}) collective-permute-start(bf16[12,512,128]{2,1,0:T(8,128)(2,1)S(1)} %shard_map.95.sent), channel_id=1, source_target_pairs={{0,1},{1,0},{2,3},{3,2},{4,5},{5,4},{6,7},{7,6},{8,9},{9,8},{10,11... | collective-permute-start | bytes 4718600 | tf_op jit(solution)/shard_map/ppermute | solution.py:29
  79.2 5.1 %shard_map.94.mine = bf16[4,512,128]{2,1,0:T(8,128)(2,1)S(1)} custom-call(bf16[4,1024,128]{2,1,0:T(8,128)(2,1)S(1)} %get-tuple-element.37.q, bf16[4,1536,128]{2,1,0:T(8,128)(2,1)S(1)} %get-tuple-element.38.k, bf16[4,1536,128]{2,1,0:T(8,128)(2,1)S(1)} %get-tuple-element.39.v), custom_call_target="tpu_custom_call" | custom-call | flops 8000000000 | bytes 1048576 | tf_op jit(solution)/shard_map/pallas_call | solution.py:403
  84.3 0.0 collective-permute-done.10.theirs
  84.3 2.1 %shard_map.96 = bf16[512,1024]{1,0:T(8,128)(2,1)} custom-call(bf16[4,512,128]{2,1,0:T(8,128)(2,1)S(1)} %shard_map.94.mine, bf16[12,512,128]{2,1,0:T(8,128)(2,1)S(1)} %shard_map.95.sent, bf16[12,512,128]{2,1,0:T(8,128)(2,1)S(1)} %collective-permute-done.10.theirs), custom_call_target="tpu_custom_call" | custom-call | flops 1000000000 | bytes 1048576 | tf_op jit(solution)/shard_map/pallas_call | solution.py:408
  (5 shorter events, 0.1 us)
Async XLA Ops:
  2.2 20.3 %collective-permute-start.6 = (bf16[64,2048]{1,0:T(8,128)(2,1)S(1)}, bf16[64,2048]{1,0:T(8,128)(2,1)S(1)}, u32[]{:S(2)}, u32[]{:S(2)}) collective-permute-start(bf16[64,2048]{1,0:T(8,128)(2,1)S(1)} %get-tuple-element.32), channel_id=1, source_target_pairs={{0,64},{1,257},{2,66},{3,259},{4,68},{5,261},{6,70},{7,263},{8,72}... | collective-permute-start | bytes 786440 | tf_op jit(solution)/shard_map/ppermute | solution.py:29
  4.7 17.8 %collective-permute-start.5 = (bf16[64,2048]{1,0:T(8,128)(2,1)S(1)}, bf16[64,2048]{1,0:T(8,128)(2,1)S(1)}, u32[]{:S(2)}, u32[]{:S(2)}) collective-permute-start(bf16[64,2048]{1,0:T(8,128)(2,1)S(1)} %get-tuple-element.32), channel_id=1, source_target_pairs={{0,96},{1,387},{2,98},{3,385},{4,100},{5,391},{6,102},{7,389},{8,1... | collective-permute-start | bytes 786440 | tf_op jit(solution)/shard_map/ppermute | solution.py:29
  6.6 15.8 %collective-permute-start.4 = (bf16[64,2048]{1,0:T(8,128)(2,1)S(1)}, bf16[64,2048]{1,0:T(8,128)(2,1)S(1)}, u32[]{:S(2)}, u32[]{:S(2)}) collective-permute-start(bf16[64,2048]{1,0:T(8,128)(2,1)S(1)} %get-tuple-element.32), channel_id=1, source_target_pairs={{0,32},{1,129},{2,34},{3,131},{4,36},{5,133},{6,38},{7,135},{8,40}... | collective-permute-start | bytes 786440 | tf_op jit(solution)/shard_map/ppermute | solution.py:29
  9.9 18.5 %collective-permute-start = (bf16[100,1024]{1,0:T(8,128)(2,1)S(1)}, bf16[100,1024]{1,0:T(8,128)(2,1)S(1)}, u32[]{:S(2)}, u32[]{:S(2)}) collective-permute-start(bf16[100,1024]{1,0:T(8,128)(2,1)S(1)} %get-tuple-element.21), channel_id=1, source_target_pairs={{0,31},{1,2},{2,1},{3,4},{4,3},{5,6},{6,5},{7,8},{8,7},{9,10},{10,... | collective-permute-start | bytes 614408 | tf_op jit(solution)/shard_map/ppermute | solution.py:52
  17.1 11.3 %collective-permute-start.1 = (bf16[100,1024]{1,0:T(8,128)(2,1)S(1)}, bf16[100,1024]{1,0:T(8,128)(2,1)S(1)}, u32[]{:S(2)}, u32[]{:S(2)}) collective-permute-start(bf16[100,1024]{1,0:T(8,128)(2,1)S(1)} %get-tuple-element.22), channel_id=1, source_target_pairs={{0,1},{1,0},{2,3},{3,2},{4,5},{5,4},{6,7},{7,6},{8,9},{9,8},{10,11... | collective-permute-start | bytes 614408 | tf_op jit(solution)/shard_map/ppermute | solution.py:29
  19.1 0.9 %copy-start = (bf16[100,1024]{1,0:T(8,128)(2,1)S(1)}, bf16[100,1024]{1,0:T(8,128)(2,1)}, u32[]{:S(2)}) copy-start(bf16[100,1024]{1,0:T(8,128)(2,1)} %w_in.1) | copy-start | bytes 614404
  20.0 0.7 copy-start.3
  20.7 7.7 %copy-start.1 = (bf16[32,16,128]{2,1,0:T(8,128)(2,1)S(1)}, bf16[32,16,128]{2,1,0:T(8,128)(2,1)}, u32[]{:S(2)}) copy-start(bf16[32,16,128]{2,1,0:T(8,128)(2,1)} %weight.3) | copy-start | bytes 393220
  20.7 7.8 %copy-start.2 = (s32[32,128]{1,0:T(8,128)S(1)}, s32[32,128]{1,0:T(8,128)}, u32[]{:S(2)}) copy-start(s32[32,128]{1,0:T(8,128)} %index.3) | copy-start | bytes 49156
  22.5 32.2 %collective-permute-start.8 = (bf16[256,2048]{1,0:T(8,128)(2,1)S(1)}, bf16[256,2048]{1,0:T(8,128)(2,1)S(1)}, u32[]{:S(2)}, u32[]{:S(2)}) collective-permute-start(bf16[256,2048]{1,0:T(8,128)(2,1)S(1)} %constant_dynamic-update-slice_fusion.here.refs_0_), channel_id=1, source_target_pairs={{0,386},{1,97},{2,384},{3,99},{4,390},{5,101},{6,388},{7,103},{8,3... | collective-permute-start | bytes 3145736 | tf_op jit(solution)/shard_map/ppermute | solution.py:29
  26.5 28.2 %collective-permute-start.7 = (bf16[256,2048]{1,0:T(8,128)(2,1)S(1)}, bf16[256,2048]{1,0:T(8,128)(2,1)S(1)}, u32[]{:S(2)}, u32[]{:S(2)}) collective-permute-start(bf16[256,2048]{1,0:T(8,128)(2,1)S(1)} %constant_dynamic-update-slice_fusion.here.refs_0_), channel_id=1, source_target_pairs={{0,128},{1,33},{2,130},{3,35},{4,132},{5,37},{6,134},{7,39},{8,136... | collective-permute-start | bytes 3145736 | tf_op jit(solution)/shard_map/ppermute | solution.py:29
  31.6 17.6 %collective-permute-start.2 = (bf16[256,128]{1,0:T(8,128)(2,1)S(1)}, bf16[256,128]{1,0:T(8,128)(2,1)S(1)}, u32[]{:S(2)}, u32[]{:S(2)}) collective-permute-start(bf16[256,128]{1,0:T(8,128)(2,1)S(1)} %get-tuple-element.25), channel_id=1, source_target_pairs={{0,31},{1,2},{2,1},{3,4},{4,3},{5,6},{6,5},{7,8},{8,7},{9,10},{10,... | collective-permute-start | bytes 196616 | tf_op jit(solution)/shard_map/ppermute | solution.py:52
  42.3 17.3 %collective-permute-start.9 = (bf16[256,2048]{1,0:T(8,128)(2,1)S(1)}, bf16[256,2048]{1,0:T(8,128)(2,1)S(1)}, u32[]{:S(2)}, u32[]{:S(2)}) collective-permute-start(bf16[256,2048]{1,0:T(8,128)(2,1)S(1)} %constant_dynamic-update-slice_fusion.here.refs_0_), channel_id=1, source_target_pairs={{0,256},{1,65},{2,258},{3,67},{4,260},{5,69},{6,262},{7,71},{8,264... | collective-permute-start | bytes 3145736 | tf_op jit(solution)/shard_map/ppermute | solution.py:29
  49.2 4.1 %collective-permute-start.3 = (bf16[768,128]{1,0:T(8,128)(2,1)S(1)}, bf16[768,128]{1,0:T(8,128)(2,1)S(1)}, u32[]{:S(2)}, u32[]{:S(2)}) collective-permute-start(bf16[768,128]{1,0:T(8,128)(2,1)S(1)} %pad_maximum_fusion.packed), channel_id=1, source_target_pairs={{0,1},{1,0},{2,3},{3,2},{4,5},{5,4},{6,7},{7,6},{8,9},{9,8},{10,11... | collective-permute-start | bytes 589832 | tf_op jit(solution)/shard_map/ppermute | solution.py:29
  67.1 17.2 %collective-permute-start.10 = (bf16[12,512,128]{2,1,0:T(8,128)(2,1)S(1)}, bf16[12,512,128]{2,1,0:T(8,128)(2,1)S(1)}, u32[]{:S(2)}, u32[]{:S(2)}) collective-permute-start(bf16[12,512,128]{2,1,0:T(8,128)(2,1)S(1)} %shard_map.95.sent), channel_id=1, source_target_pairs={{0,1},{1,0},{2,3},{3,2},{4,5},{5,4},{6,7},{7,6},{8,9},{9,8},{10,11... | collective-permute-start | bytes 4718600 | tf_op jit(solution)/shard_map/ppermute | solution.py:29
